TPU v7x, 32 devices: a 4x4x1 block of a 4x4x8 slice. The times are simulated.
32 devices in a mesh: dp: 1 (over z), tp: 4 (over y), dm: 8 (over x, core).
Axes of the slice: x: 4, y: 4, z: 1, core: 2. Of those that a mesh axis runs over, the one named last changes fastest.
The devices are a block of a 4x4x8 slice.
Arguments:
- x_in: bfloat16 [2048, 5120], P('dp', 'dm')
- positions: int32 [2048], P(('dp', 'dm'))
- k_cache: bfloat16 [2048, 8, 64, 160], P(('dp', 'dm'), 'tp')
- v_cache: bfloat16 [2048, 8, 64, 160], P(('dp', 'dm'), 'tp')
- ln_gain: bfloat16 [5120], P('dm')
- w_q: bfloat16 [5120, 5120], P('dm', 'tp')
- w_k: bfloat16 [5120, 1280], P('dm', 'tp')
- w_v: bfloat16 [5120, 1280], P('dm', 'tp')
- w_gate: bfloat16 [5120, 13824], P('dm', 'tp')
- w_up: bfloat16 [5120, 13824], P('dm', 'tp')
- q_gain: bfloat16 [32, 160], P('tp')
- k_gain: bfloat16 [8, 160], P('tp')
- w_out: bfloat16 [5120, 5120], P('tp', 'dm')
- w_down: bfloat16 [13824, 5120], P('tp', 'dm')
Outputs:
- output 1: bfloat16 [2048, 5120], P('dp', 'dm')
- output 2: bfloat16 [2048, 8, 160], P(('dp', 'dm'), 'tp')
- output 3: bfloat16 [2048, 8, 160], P(('dp', 'dm'), 'tp')
All inputs are finite; a program needn't handle non-finite values.
Results may differ from a plain program's by a relative error of at most 0.0139342.
Values are sent between devices in bfloat16 or wider.
A program may use at most 768 MiB of HBM per device.

v0:
```python
import jax
import jax.numpy as jnp
from jax import lax
from jax.sharding import PartitionSpec as P

NORM_EPS = 1e-5
ROPE_THETA = 75000000.0


def layer_norm_last(values, gain_w):
    centred = values - jnp.mean(values, axis=-1, keepdims=True)
    spread = jnp.mean(centred * centred, axis=-1, keepdims=True)
    return centred * lax.rsqrt(spread + NORM_EPS) * gain_w


def rotary(values, positions):
    head_dim = values.shape[-1]
    inv_freq = ROPE_THETA ** (-jnp.arange(0, head_dim, 2, dtype=jnp.float32) / head_dim)
    angles = positions.astype(jnp.float32)[:, None] * inv_freq[None, :]
    cos_a = jnp.cos(angles)[:, None, :]
    sin_a = jnp.sin(angles)[:, None, :]
    pair_view = values.reshape(values.shape[:-1] + (head_dim // 2, 2))
    even_part = pair_view[..., 0]
    odd_part = pair_view[..., 1]
    turned = jnp.stack([even_part * cos_a - odd_part * sin_a, odd_part * cos_a + even_part * sin_a], axis=-1)
    return turned.reshape(values.shape)


def attend(q_rot, k_rot, v_new, k_cache, v_cache, positions):
    score_scale = q_rot.shape[-1] ** -0.5
    s_cache = jnp.einsum('rkgd,rksd->rkgs', q_rot, k_cache, preferred_element_type=jnp.float32) * score_scale
    key_valid = jnp.arange(k_cache.shape[2])[None, None, None, :] < positions[:, None, None, None]
    s_cache = jnp.where(key_valid, s_cache, -1e30)
    s_new = jnp.einsum('rkgd,rkd->rkg', q_rot, k_rot, preferred_element_type=jnp.float32) * score_scale
    row_max = jnp.maximum(jnp.max(s_cache, axis=-1), s_new)
    p_cache = jnp.exp(s_cache - row_max[..., None])
    p_new = jnp.exp(s_new - row_max)
    denom_sum = jnp.sum(p_cache, axis=-1) + p_new
    numer_acc = jnp.einsum('rkgs,rksd->rkgd', p_cache.astype(jnp.bfloat16), v_cache, preferred_element_type=jnp.float32)
    numer_acc = numer_acc + p_new[..., None] * v_new.astype(jnp.float32)[:, :, None, :]
    return (numer_acc / denom_sum[..., None]).astype(jnp.bfloat16)


def solution(mesh):
    dm_size = mesh.shape['dm']
    x_spec = P('dp', 'dm')
    row_spec = P(('dp', 'dm'))
    cache_spec = P(('dp', 'dm'), 'tp', None, None)
    new_spec = P(('dp', 'dm'), 'tp', None)
    hid_tp = P('dm', 'tp')
    tp_hid = P('tp', 'dm')
    head_spec = P('tp', None)

    def device_step(x_in, positions, k_cache, v_cache, ln_gain, w_q, w_k, w_v, w_gate, w_up, q_gain, k_gain, w_out, w_down):
        rows_loc = k_cache.shape[0]
        kv_loc = k_cache.shape[1]
        head_dim = k_cache.shape[3]
        heads_loc = q_gain.shape[0]
        d_model = x_in.shape[1] * dm_size
        x_f32 = x_in.astype(jnp.float32)
        row_mean = lax.psum(jnp.sum(x_f32, axis=1, keepdims=True), 'dm') / d_model
        centred = x_f32 - row_mean
        row_var = lax.psum(jnp.sum(centred * centred, axis=1, keepdims=True), 'dm') / d_model
        normed = (centred * lax.rsqrt(row_var + NORM_EPS) * ln_gain.astype(jnp.float32)).astype(jnp.bfloat16)
        part_q = jnp.dot(normed, w_q, preferred_element_type=jnp.float32).astype(jnp.bfloat16)
        part_k = jnp.dot(normed, w_k, preferred_element_type=jnp.float32).astype(jnp.bfloat16)
        part_v = jnp.dot(normed, w_v, preferred_element_type=jnp.float32).astype(jnp.bfloat16)
        part_g = jnp.dot(normed, w_gate, preferred_element_type=jnp.float32).astype(jnp.bfloat16)
        part_u = jnp.dot(normed, w_up, preferred_element_type=jnp.float32).astype(jnp.bfloat16)
        sum_q, sum_k, sum_v, sum_g, sum_u = lax.psum((part_q, part_k, part_v, part_g, part_u), 'dm')
        row_start = lax.axis_index('dm') * rows_loc
        q_rows = lax.dynamic_slice_in_dim(sum_q, row_start, rows_loc, axis=0)
        k_rows = lax.dynamic_slice_in_dim(sum_k, row_start, rows_loc, axis=0)
        v_rows = lax.dynamic_slice_in_dim(sum_v, row_start, rows_loc, axis=0)
        q_heads = layer_norm_last(q_rows.reshape(rows_loc, heads_loc, head_dim).astype(jnp.float32), q_gain.astype(jnp.float32))
        q_rot = rotary(q_heads, positions).astype(jnp.bfloat16).reshape(rows_loc, kv_loc, heads_loc // kv_loc, head_dim)
        k_heads = layer_norm_last(k_rows.reshape(rows_loc, kv_loc, head_dim).astype(jnp.float32), k_gain.astype(jnp.float32))
        k_new = rotary(k_heads, positions).astype(jnp.bfloat16)
        v_new = v_rows.reshape(rows_loc, kv_loc, head_dim)
        attn_loc = attend(q_rot, k_new, v_new, k_cache, v_cache, positions).reshape(rows_loc, heads_loc * head_dim)
        attn_all = lax.all_gather(attn_loc, 'dm', axis=0, tiled=True)
        mlp_act = (jax.nn.silu(sum_g.astype(jnp.float32)) * sum_u.astype(jnp.float32)).astype(jnp.bfloat16)
        part_out = jnp.dot(attn_all, w_out, preferred_element_type=jnp.float32) + jnp.dot(mlp_act, w_down, preferred_element_type=jnp.float32)
        out_sum = lax.psum(part_out.astype(jnp.bfloat16), 'tp')
        x_out = (x_f32 + out_sum.astype(jnp.float32)).astype(jnp.bfloat16)
        return x_out, k_new, v_new

    return jax.shard_map(
        device_step,
        mesh=mesh,
        in_specs=(x_spec, row_spec, cache_spec, cache_spec, P('dm'), hid_tp, hid_tp, hid_tp, hid_tp, hid_tp, head_spec, head_spec, tp_hid, tp_hid),
        out_specs=(x_spec, new_spec, new_spec),
        check_vma=False,
    )
```

profile of v0, /device:TPU:97, one launch (start us, length us, event | category | flops | bytes accessed | tf_op | source)
XLA Modules:
  0.0 630.4 jit_solution(377913121132475731)
XLA Ops:
  7.3 2.3 convert_reduce_fusion
  9.5 14.1 %psum.56 = f32[2048,1]{0,1:T(1,128)S(1)} all-reduce(f32[2048,1]{0,1:T(1,128)S(1)} %bitcast.50), channel_id=1, replica_groups=mesh['dp'=1,'tp'=4,'dm'=8] {'dm'}, use_global_device_ids=true, to_apply=%region_1.0 | all-reduce | flops 2048 | bytes 16384 | tf_op jit(solution)/shard_map/psum | solution.py:61
  23.6 2.7 fusion.9
  26.3 14.8 %psum.57 = f32[2048,1]{0,1:T(1,128)S(1)} all-reduce(f32[2048,1]{0,1:T(1,128)S(1)} %bitcast.51), channel_id=1, replica_groups=mesh['dp'=1,'tp'=4,'dm'=8] {'dm'}, use_global_device_ids=true, to_apply=%region_3.0 | all-reduce | flops 2048 | bytes 16384 | tf_op jit(solution)/shard_map/psum | solution.py:63
  41.2 17.6 %convolution_convert_fusion = bf16[2048,3456]{1,0:T(8,128)(2,1)} fusion(bf16[640,3456]{1,0:T(8,128)(2,1)} %param.23, bf16[2048,640]{1,0:T(8,128)(2,1)} %param.14, f32[640]{0:T(1024)S(1)} %convert_element_type.95, f32[2048]{0:T(1024)S(1)} %bitcast.52, f32[2048]{0:T(1024)S(1)} %bitcast.45), kind=kOutput, calls=%fused_computation.7 | convolution fusion | flops 9073328128 | bytes 21219840 | tf_op jit(solution)/shard_map/dot_general | solution.py:69
  58.8 17.1 %convolution_convert_fusion.1 = bf16[2048,3456]{1,0:T(8,128)(2,1)} fusion(bf16[640,3456]{1,0:T(8,128)(2,1)} %param.22, bf16[2048,640]{1,0:T(8,128)(2,1)S(1)} %copy-done.2, f32[640]{0:T(1024)S(1)} %convert_element_type.95, f32[2048]{0:T(1024)S(1)} %bitcast.53, f32[2048]{0:T(1024)S(1)} %bitcast.46), kind=kOutput, calls=%fused_computation.8 | convolution fusion | flops 9073328128 | bytes 21219840 | tf_op jit(solution)/shard_map/dot_general | solution.py:68
  75.9 6.3 convolution_convert_fusion.2
  82.2 2.8 convolution_convert_fusion.3
  85.0 2.7 convolution_convert_fusion.4
  87.9 0.5 copy-done.7
  88.4 0.1 reshape.153
  88.6 0.1 copy.24
  88.7 0.5 copy.25
  89.2 23.0 %copy.27 = bf16[256,2,64,160]{3,2,1,0:T(8,128)(2,1)} copy(bf16[256,2,64,160]{0,3,2,1:T(8,128)(2,1)} %param.16) | data formatting | bytes 20971520 | tf_op args[2]
  112.2 23.1 %copy.28 = bf16[256,2,64,160]{3,2,1,0:T(8,128)(2,1)} copy(bf16[256,2,64,160]{0,3,2,1:T(8,128)(2,1)} %param.17) | data formatting | bytes 20971520 | tf_op args[3]
  135.3 0.1 iota_compare_fusion
  135.4 0.4 multiply_cosine_fusion
  135.8 312.2 %all-reduce.6.cloned.1.call-done = (bf16[2048,1280]{1,0:T(8,128)(2,1)}, bf16[2048,320]{0,1:T(8,128)(2,1)}, bf16[2048,320]{0,1:T(8,128)(2,1)}, bf16[2048,3456]{1,0:T(8,128)(2,1)}, bf16[2048,3456]{1,0:T(8,128)(2,1)}) async-done(((bf16[2048,1280]{1,0:T(8,128)(2,1)}, bf16[2048,320]{0,1:T(8,128)(2,1)}, bf16[2048,320]{0,1:T(8,128)(2,1)}, bf16[2048,3456]{1,0:T(8,128)(2,1)}, bf16[2048,3456]{1,0:T(8,128)(2,1)}), ...) | async-done | bytes 36175888 | tf_op jit(solution)/shard_map/psum | solution.py:70
  448.0 1.0 dynamic-slice_convert_fusion.1
  449.0 0.2 reshape.151
  449.3 0.2 multiply_multiply_fusion.1
  449.6 0.4 subtract_convert_fusion.1
  450.0 0.4 pad_maximum_fusion.1
  450.5 1.1 copy.31
  451.6 1.2 dynamic-slice_convert_fusion
  452.8 0.4 copy.22
  453.2 0.8 reshape.148
  453.9 0.1 reduce_sum.65
  454.1 0.1 multiply_reduce_fusion
  454.2 0.9 multiply_multiply_fusion
  455.1 1.8 subtract_convert_fusion
  456.9 1.5 pad_maximum_fusion
  458.4 0.2 convert_element_type.103
  458.7 1.0 copy.26
  459.7 1.8 fusion.29
  461.5 8.3 %fusion.28 = (f32[256,2,4]{2,1,0:T(2,128)S(1)}, f32[256,2,4,64]{3,2,1,0:T(4,128)S(1)}) fusion(bf16[256,2,4,160]{3,2,1,0:T(4,128)(2,1)S(1)} %copy.26, bf16[256,2,64,160]{3,2,1,0:T(8,128)(2,1)} %copy.27, pred[256,64]{1,0:T(8,128)(4,1)S(1)} %iota_compare_fusion), kind=kOutput, calls=%fused_computation.58 | convolution fusion | flops 42334208 | bytes 11689984 | tf_op jit(solution)/shard_map/rkgd,rksd->rkgs/dot_general | solution.py:31
  469.8 0.2 multiply_maximum_fusion
  469.9 1.4 fusion.17
  471.4 1.1 fusion.27
  472.5 0.9 copy.29
  473.4 7.6 %fusion.15 = bf16[256,2,4,160]{3,2,1,0:T(4,128)(2,1)S(1)} fusion(bf16[256,2,64,160]{3,2,1,0:T(8,128)(2,1)} %copy.28, f32[256,2,4]{2,1,0:T(2,128)} %get-tuple-element.8, f32[256,2,160]{2,1,0:T(2,128)} %copy.29, f32[256,2,4]{2,1,0:T(2,128)} %get-tuple-element.9, f32[256,2,4,64]{3,2,1,0:T(4,128)S(1)} %get-tuple-element.17, ...), kind=kOutput, calls=%fused_computation.24 | convolution fusion | flops 43515904 | bytes 12017664 | tf_op jit(solution)/shard_map/rkgs,rksd->rkgd/dot_general | solution.py:39
  481.1 1.5 copy.30
  482.7 37.3 %all-gather.2.cloned.1.call-done = bf16[2048,1280]{0,1:T(8,128)(2,1)} async-done(((bf16[256,1280]{0,1:T(8,128)(2,1)}), bf16[2048,1280]{0,1:T(8,128)(2,1)}) %all-gather.2.cloned.1.call-update) | async-done | bytes 5242896 | tf_op jit(solution)/shard_map/all_gather | solution.py:81
  520.0 9.6 %fusion.30 = f32[2048,640]{1,0:T(8,128)} fusion(bf16[2048,1280]{0,1:T(8,128)(2,1)} %all-gather.2.cloned.1.call-done, bf16[1280,640]{1,0:T(8,128)(2,1)} %param.26), kind=kOutput, calls=%fused_computation.60 | convolution fusion | flops 3355443200 | bytes 12124160 | tf_op jit(solution)/shard_map/dot_general | solution.py:83
  529.6 26.6 %add_convert_fusion = bf16[2048,640]{1,0:T(8,128)(2,1)} fusion(f32[2048,640]{1,0:T(8,128)} %fusion.30, bf16[3456,640]{1,0:T(8,128)(2,1)} %param.27, bf16[2048,3456]{1,0:T(8,128)(2,1)} %get-tuple-element.6, bf16[2048,3456]{1,0:T(8,128)(2,1)} %get-tuple-element.7), kind=kOutput, calls=%fused_computation.20 | convolution fusion | flops 9118941184 | bytes 40599552 | tf_op jit(solution)/shard_map/dot_general | solution.py:83
  556.4 0.7 convert_element_type.109
  557.1 61.6 %all-reduce.4.cloned.1.call-done = bf16[2048,640]{1,0:T(8,128)(2,1)} async-done(((bf16[2048,640]{1,0:T(8,128)(2,1)}), bf16[2048,640]{1,0:T(8,128)(2,1)}) %all-reduce.4.cloned.1.call-update) | async-done | bytes 2621456 | tf_op jit(solution)/shard_map/psum | solution.py:84
  618.7 4.7 fusion.12
  (37 shorter events, 0.6 us)
Async XLA Ops:
  7.2 68.7 %copy-start = (bf16[640,1280]{1,0:T(8,128)(2,1)S(1)}, bf16[640,1280]{1,0:T(8,128)(2,1)}, u32[]{:S(2)}) copy-start(bf16[640,1280]{1,0:T(8,128)(2,1)} %param.19) | copy-start | bytes 4915204
  7.2 33.9 %copy-start.6 = (bf16[640]{0:T(1024)(128)(2,1)S(1)}, bf16[640]{0:T(1024)(128)(2,1)}, u32[]{:S(2)}) copy-start(bf16[640]{0:T(1024)(128)(2,1)} %param.18) | copy-start | bytes 3844
  7.2 440.8 %all-reduce.6.cloned.1.call-start = ((), (), s32[]{:S(2)}) async-start(), calls=%async_computation.2 | async-start | bytes 72351744 | tf_op jit(solution)/shard_map/psum | solution.py:70
  41.2 17.7 %copy-start.2 = (bf16[2048,640]{1,0:T(8,128)(2,1)S(1)}, bf16[2048,640]{1,0:T(8,128)(2,1)}, u32[]{:S(2)}) copy-start(bf16[2048,640]{1,0:T(8,128)(2,1)} %param.14) | copy-start | bytes 7864324
  75.9 6.3 copy-start.8
  82.2 2.8 copy-start.9
  87.7 0.7 copy-start.7
  87.7 0.8 copy-start.4
  87.7 0.8 copy-start.5
  87.8 432.2 %all-gather.2.cloned.1.call-start = ((), (), s32[]{:S(2)}) async-start(), calls=%async_computation | async-start | bytes 5898240 | tf_op jit(solution)/shard_map/all_gather | solution.py:81
  449.0 23.5 %copy-start.3 = (bf16[256,320]{0,1:T(8,128)(2,1)}, bf16[256,320]{0,1:T(8,128)(2,1)S(1)}, u32[]{:S(2)}) copy-start(bf16[256,320]{0,1:T(8,128)(2,1)S(1)} %get-tuple-element.19) | copy-start | bytes 491524
  482.6 136.1 %all-reduce.4.cloned.1.call-start = ((), (), s32[]{:S(2)}) async-start(), calls=%async_computation.1 | async-start | bytes 5242880 | tf_op jit(solution)/shard_map/psum | solution.py:84
  556.3 67.1 %copy-start.1 = (bf16[640,1280]{1,0:T(8,128)(2,1)S(1)}, bf16[640,1280]{1,0:T(8,128)(2,1)}, u32[]{:S(2)}) copy-start(bf16[640,1280]{1,0:T(8,128)(2,1)} %param.19) | copy-start | bytes 4915204
Sparse Core Ops, SparseCore 0:
  87.9 360.0 all-reduce.5
  482.8 37.2 all-gather.1
  556.5 62.2 all-reduce.3
where the time goes:
time: 641 us; the launch traced here: 630 us
  waiting for transfers between devices  411 us (64%)
  matrix products  100 us (16%)
  local copies, waits for them, and re-layouts  54.4 us (8%)
  blocking collectives  28.8 us (4%)
  other arithmetic  20.7 us (3%)
  between operations  14.5 us (2%)
    psum x1, waiting for transfers between devices, device_step(): lax.psum((part_q, part_k, part_v, part_g, part_u), 'dm')  312 us
    psum x1, waiting for transfers between devices, device_step(): out_sum = lax.psum(part_out.astype(jnp.bfloat16), 'tp')  61.6 us
    unnamed x22, local copies, waits for them, and re-layouts  46.7 us
    all_gather x1, waiting for transfers between devices, device_step(): attn_all = lax.all_gather(attn_loc, 'dm', axis=0, tiled=True)  37.3 us
    dot_general x1, matrix products, device_step(): jnp.dot(mlp_act, w_down, preferred_element_type=jnp.float32)  26.6 us
    dot_general x1, matrix products, device_step(): jnp.dot(normed, w_up, preferred_element_type=jnp.float32)  17.6 us
    dot_general x1, matrix products, device_step(): jnp.dot(normed, w_gate, preferred_element_type=jnp.float32)  17.1 us
    psum x1, blocking collectives, device_step(): lax.psum(jnp.sum(centred * centred, axis=1, keepdims=True), 'dm') / d_model  14.8 us
  transfers between devices with their start and end apart: 3, of which 3 were waited for; matrix products, arithmetic and copies ran while one was open for 8% of the time, Pallas kernels for 0%

commit v1 on v0

--- a/solution.py
+++ b/solution.py
@@ -1,10 +1,19 @@
+import functools
+
 import jax
 import jax.numpy as jnp
 from jax import lax
+from jax.experimental import pallas as pl
+from jax.experimental.pallas import tpu as pltpu
 from jax.sharding import PartitionSpec as P
 
 NORM_EPS = 1e-5
 ROPE_THETA = 75000000.0
+MESH = pl.DeviceIdType.MESH
+BF16 = jnp.bfloat16
+F32 = jnp.float32
+ANY = pl.ANY
+VMEM_LIMIT = 66 * 1024 * 1000 - 1024 * 600
 
 
 def layer_norm_last(values, gain_w):
@@ -24,6 +33,200 @@
     odd_part = pair_view[..., 1]
     turned = jnp.stack([even_part * cos_a - odd_part * sin_a, odd_part * cos_a + even_part * sin_a], axis=-1)
     return turned.reshape(values.shape)
+
+
+def project_kernel(nx, ntile, x_ref, wq_ref, wk_ref, wv_ref, wg_ref, wu_ref,
+                   q_out, k_out, v_out, act_out,
+                   xbuf, bq, bk, bv, bg, bu, rq, rk, rg, lq, lv, lu,
+                   x_loc, x_snd, x_rcv, w_loc, w_snd, w_rcv, r_snd, r_rcv):
+    dm = lax.axis_index('dm')
+    xi = dm // 2
+    core = lax.rem(dm, 2)
+    other = 2 * xi + 1 - core
+    right = lax.rem(xi + 1, nx) * 2 + core
+    left = lax.rem(xi + nx - 1, nx) * 2 + core
+    rb = xbuf.shape[1]
+    hid = x_ref.shape[1]
+    tw = wg_ref.shape[1] // ntile
+
+    pieces = [(wq_ref, bq, None), (wk_ref, bk, None), (wv_ref, bv, None)]
+    for t in range(ntile):
+        pieces.append((wg_ref, bg, pl.ds(t * tw, tw)))
+        pieces.append((wu_ref, bu, pl.ds(t * tw, tw)))
+
+    def x_local(j):
+        return pltpu.make_async_copy(
+            x_ref.at[pl.ds((2 * j + core) * rb, rb), :], xbuf.at[j, :, pl.ds(0, hid)], x_loc.at[j])
+
+    def x_remote(j):
+        return pltpu.make_async_remote_copy(
+            src_ref=x_ref.at[pl.ds((2 * j + 1 - core) * rb, rb), :], dst_ref=xbuf.at[j, :, pl.ds(hid, hid)],
+            send_sem=x_snd.at[j], recv_sem=x_rcv.at[j], device_id={'dm': other}, device_id_type=MESH)
+
+    def w_local(n):
+        src, dst, cols = pieces[n]
+        if cols is None:
+            return pltpu.make_async_copy(src, dst.at[pl.ds(0, hid), :], w_loc.at[n])
+        return pltpu.make_async_copy(src.at[:, cols], dst.at[pl.ds(0, hid), cols], w_loc.at[n])
+
+    def w_remote(n):
+        src, dst, cols = pieces[n]
+        if cols is not None:
+            src = src.at[:, cols]
+            dst = dst.at[pl.ds(hid, hid), cols]
+        else:
+            dst = dst.at[pl.ds(hid, hid), :]
+        return pltpu.make_async_remote_copy(
+            src_ref=src, dst_ref=dst, send_sem=w_snd.at[n], recv_sem=w_rcv.at[n],
+            device_id={'dm': other}, device_id_type=MESH)
+
+    barrier = pltpu.get_barrier_semaphore()
+    for peer in (other, right, left):
+        pl.semaphore_signal(barrier, inc=1, device_id={'dm': peer}, device_id_type=MESH)
+    pl.semaphore_wait(barrier, 3)
+
+    for j in range(nx):
+        x_local(j).start()
+        x_remote(j).start()
+    for n in range(len(pieces)):
+        w_local(n).start()
+        w_remote(n).start()
+
+    for ref in (rq, rk, rg, lq, lv, lu):
+        ref[0] = jnp.zeros(ref.shape[1:], ref.dtype)
+
+    for j in range(nx):
+        x_local(j).wait()
+        x_remote(j).wait()
+
+    def hop(d, t, s, slot, cols):
+        nxt = jnp.minimum(s + 1, nx - 1)
+        return pltpu.make_async_remote_copy(
+            src_ref=slot.at[s, :, cols], dst_ref=slot.at[nxt, :, cols],
+            send_sem=r_snd.at[d, t, s], recv_sem=r_rcv.at[d, t, nxt],
+            device_id={'dm': left if d else right}, device_id_type=MESH)
+
+    def arrived(d, t, s, slot, cols):
+        return pltpu.make_async_remote_copy(
+            src_ref=slot.at[s, :, cols], dst_ref=slot.at[s, :, cols],
+            send_sem=r_snd.at[d, t, s], recv_sem=r_rcv.at[d, t, s],
+            device_id={'dm': left if d else right}, device_id_type=MESH)
+
+    def tile(d, t, s, weight, w_cols, slot, cols):
+        row = lax.rem(xi + 1 + s, nx) if d else lax.rem(xi + 2 * nx - 1 - s, nx)
+        part = jnp.dot(xbuf[row], weight[:, w_cols], preferred_element_type=F32)
+
+        @pl.when(s > 0)
+        def _():
+            arrived(d, t, s, slot, cols).wait_recv()
+
+        slot[s, :, cols] = (part + slot[s, :, cols].astype(F32)).astype(BF16)
+
+        @pl.when(s < nx - 1)
+        def _():
+            hop(d, t, s, slot, cols).start()
+
+    def wait_piece(n):
+        w_local(n).wait()
+        w_remote(n).wait()
+
+    half = rq.shape[2]
+    kw = rk.shape[2]
+
+    def step(s, carry):
+        @pl.when(s == 0)
+        def _():
+            wait_piece(0)
+
+        tile(0, 0, s, bq, pl.ds(0, half), rq, pl.ds(0, half))
+        tile(1, 0, s, bq, pl.ds(half, half), lq, pl.ds(0, half))
+
+        @pl.when(s == 0)
+        def _():
+            wait_piece(1)
+            wait_piece(2)
+
+        tile(0, 1, s, bk, pl.ds(0, kw), rk, pl.ds(0, kw))
+        tile(1, 1, s, bv, pl.ds(0, kw), lv, pl.ds(0, kw))
+        for t in range(ntile):
+            @pl.when(s == 0)
+            def _():
+                wait_piece(3 + 2 * t)
+                wait_piece(4 + 2 * t)
+
+        def mlp(t, inner):
+            cols = pl.ds(pl.multiple_of(t * tw, 128), tw)
+            tile(0, 2 + t, s, bg, cols, rg, cols)
+            tile(1, 2 + t, s, bu, cols, lu, cols)
+
+            @pl.when(s == nx - 1)
+            def _():
+                gate = rg[nx - 1, :, cols].astype(F32)
+                up = lu[nx - 1, :, cols].astype(F32)
+                act_out[:, cols] = (gate / (1.0 + jnp.exp(-gate)) * up).astype(BF16)
+
+            return inner
+
+        return lax.fori_loop(0, ntile, mlp, carry)
+
+    lax.fori_loop(0, nx, step, 0)
+    q_out[:, :half] = rq[nx - 1]
+    q_out[:, half:] = lq[nx - 1]
+    k_out[...] = rk[nx - 1]
+    v_out[...] = lv[nx - 1]
+
+    def sent(s, carry):
+        hop(0, 0, s, rq, pl.ds(0, half)).wait_send()
+        hop(1, 0, s, lq, pl.ds(0, half)).wait_send()
+        hop(0, 1, s, rk, pl.ds(0, kw)).wait_send()
+        hop(1, 1, s, lv, pl.ds(0, kw)).wait_send()
+        for t in range(ntile):
+            cols = pl.ds(t * tw, tw)
+            hop(0, 2 + t, s, rg, cols).wait_send()
+            hop(1, 2 + t, s, lu, cols).wait_send()
+        return carry
+
+    lax.fori_loop(0, nx - 1, sent, 0)
+
+
+def project(nx, h, w_q, w_k, w_v, w_gate, w_up):
+    rows, hid = h.shape
+    rb = rows // (2 * nx)
+    nq, nk, nf = w_q.shape[1], w_k.shape[1], w_gate.shape[1]
+    ntile = 3
+    npiece = 3 + 2 * ntile
+    vmem = pl.BlockSpec(memory_space=pltpu.VMEM)
+    return pl.pallas_call(
+        functools.partial(project_kernel, nx, ntile),
+        out_shape=(jax.ShapeDtypeStruct((rb, nq), BF16), jax.ShapeDtypeStruct((rb, nk), BF16),
+                   jax.ShapeDtypeStruct((rb, nk), BF16), jax.ShapeDtypeStruct((rb, nf), BF16)),
+        in_specs=[pl.BlockSpec(memory_space=ANY)] * 6,
+        out_specs=(vmem,) * 4,
+        scratch_shapes=[
+            pltpu.VMEM((nx, rb, 2 * hid), BF16),
+            pltpu.VMEM((2 * hid, nq), BF16),
+            pltpu.VMEM((2 * hid, nk), BF16),
+            pltpu.VMEM((2 * hid, nk), BF16),
+            pltpu.VMEM((2 * hid, nf), BF16),
+            pltpu.VMEM((2 * hid, nf), BF16),
+            pltpu.VMEM((nx, rb, nq // 2), BF16),
+            pltpu.VMEM((nx, rb, nk), BF16),
+            pltpu.VMEM((nx, rb, nf), BF16),
+            pltpu.VMEM((nx, rb, nq // 2), BF16),
+            pltpu.VMEM((nx, rb, nk), BF16),
+            pltpu.VMEM((nx, rb, nf), BF16),
+            pltpu.SemaphoreType.DMA((nx,)),
+            pltpu.SemaphoreType.DMA((nx,)),
+            pltpu.SemaphoreType.DMA((nx,)),
+            pltpu.SemaphoreType.DMA((npiece,)),
+            pltpu.SemaphoreType.DMA((npiece,)),
+            pltpu.SemaphoreType.DMA((npiece,)),
+            pltpu.SemaphoreType.DMA((2, 2 + ntile, nx)),
+            pltpu.SemaphoreType.DMA((2, 2 + ntile, nx)),
+        ],
+        compiler_params=pltpu.CompilerParams(collective_id=0, has_side_effects=True, vmem_limit_bytes=VMEM_LIMIT),
+        name='project',
+    )(h, w_q, w_k, w_v, w_gate, w_up)
 
 
 def attend(q_rot, k_rot, v_new, k_cache, v_cache, positions):
@@ -43,6 +246,7 @@
 
 def solution(mesh):
     dm_size = mesh.shape['dm']
+    nx = dm_size // 2
     x_spec = P('dp', 'dm')
     row_spec = P(('dp', 'dm'))
     cache_spec = P(('dp', 'dm'), 'tp', None, None)
@@ -56,31 +260,27 @@
         kv_loc = k_cache.shape[1]
         head_dim = k_cache.shape[3]
         heads_loc = q_gain.shape[0]
-        d_model = x_in.shape[1] * dm_size
+        hid = x_in.shape[1]
+        d_model = hid * dm_size
         x_f32 = x_in.astype(jnp.float32)
-        row_mean = lax.psum(jnp.sum(x_f32, axis=1, keepdims=True), 'dm') / d_model
-        centred = x_f32 - row_mean
-        row_var = lax.psum(jnp.sum(centred * centred, axis=1, keepdims=True), 'dm') / d_model
-        normed = (centred * lax.rsqrt(row_var + NORM_EPS) * ln_gain.astype(jnp.float32)).astype(jnp.bfloat16)
-        part_q = jnp.dot(normed, w_q, preferred_element_type=jnp.float32).astype(jnp.bfloat16)
-        part_k = jnp.dot(normed, w_k, preferred_element_type=jnp.float32).astype(jnp.bfloat16)
-        part_v = jnp.dot(normed, w_v, preferred_element_type=jnp.float32).astype(jnp.bfloat16)
-        part_g = jnp.dot(normed, w_gate, preferred_element_type=jnp.float32).astype(jnp.bfloat16)
-        part_u = jnp.dot(normed, w_up, preferred_element_type=jnp.float32).astype(jnp.bfloat16)
-        sum_q, sum_k, sum_v, sum_g, sum_u = lax.psum((part_q, part_k, part_v, part_g, part_u), 'dm')
-        row_start = lax.axis_index('dm') * rows_loc
-        q_rows = lax.dynamic_slice_in_dim(sum_q, row_start, rows_loc, axis=0)
-        k_rows = lax.dynamic_slice_in_dim(sum_k, row_start, rows_loc, axis=0)
-        v_rows = lax.dynamic_slice_in_dim(sum_v, row_start, rows_loc, axis=0)
+        loc_mean = jnp.mean(x_f32, axis=1)
+        loc_cent = x_f32 - loc_mean[:, None]
+        loc_m2 = jnp.sum(loc_cent * loc_cent, axis=1)
+        stats = lax.all_gather(jnp.stack([loc_mean, loc_m2]), 'dm', axis=0)
+        row_mean = jnp.mean(stats[:, 0], axis=0)
+        diff = stats[:, 0] - row_mean[None]
+        row_var = (jnp.sum(stats[:, 1], axis=0) + hid * jnp.sum(diff * diff, axis=0)) / d_model
+        normed = ((x_f32 - row_mean[:, None]) * lax.rsqrt(row_var + NORM_EPS)[:, None] * ln_gain.astype(jnp.float32)).astype(jnp.bfloat16)
+        q_rows, k_rows, v_rows, act = project(nx, normed, w_q, w_k, w_v, w_gate, w_up)
         q_heads = layer_norm_last(q_rows.reshape(rows_loc, heads_loc, head_dim).astype(jnp.float32), q_gain.astype(jnp.float32))
         q_rot = rotary(q_heads, positions).astype(jnp.bfloat16).reshape(rows_loc, kv_loc, heads_loc // kv_loc, head_dim)
         k_heads = layer_norm_last(k_rows.reshape(rows_loc, kv_loc, head_dim).astype(jnp.float32), k_gain.astype(jnp.float32))
         k_new = rotary(k_heads, positions).astype(jnp.bfloat16)
         v_new = v_rows.reshape(rows_loc, kv_loc, head_dim)
         attn_loc = attend(q_rot, k_new, v_new, k_cache, v_cache, positions).reshape(rows_loc, heads_loc * head_dim)
+        act_all = lax.all_gather(act, 'dm', axis=0, tiled=True)
         attn_all = lax.all_gather(attn_loc, 'dm', axis=0, tiled=True)
-        mlp_act = (jax.nn.silu(sum_g.astype(jnp.float32)) * sum_u.astype(jnp.float32)).astype(jnp.bfloat16)
-        part_out = jnp.dot(attn_all, w_out, preferred_element_type=jnp.float32) + jnp.dot(mlp_act, w_down, preferred_element_type=jnp.float32)
+        part_out = jnp.dot(attn_all, w_out, preferred_element_type=jnp.float32) + jnp.dot(act_all, w_down, preferred_element_type=jnp.float32)
         out_sum = lax.psum(part_out.astype(jnp.bfloat16), 'tp')
         x_out = (x_f32 + out_sum.astype(jnp.float32)).astype(jnp.bfloat16)
         return x_out, k_new, v_new

time: 641 us -> 493 us (0.77); the launches traced: 630 us -> 491 us
  waiting for transfers between devices: 411 us -> 164 us
  Pallas kernels: 0 us -> 172 us
  matrix products: 100 us -> 43.5 us
  blocking collectives: 28.8 us -> 19 us
    psum x1 -> x0, waiting for transfers between devices: 312 us -> none  [device_step(): lax.psum((part_q, part_k, part_v, part_g, part_u), 'dm')]
    pallas_call x0 -> x1, Pallas kernels: none -> 172 us  [project(): pl.pallas_call(functools.partial(project_kernel, nx, ntile), out_shape=(j...]
    all_gather x0 -> x1, waiting for transfers between devices: none -> 64.4 us  [device_step(): act_all = lax.all_gather(act, 'dm', axis=0, tiled=True)]
    dot_general x6 -> x1, matrix products: 73.2 us -> 17.6 us  [device_step(): jnp.dot(act_all, w_down, preferred_element_type=jnp.float32)]
    psum x2 -> x0, blocking collectives: 28.8 us -> none  [the longest x1 14.8 us: device_step(): lax.psum(jnp.sum(centred * centred, axis=1, keepdims=True), 'dm') / d_model]
    all_gather x0 -> x1, blocking collectives: none -> 19 us  [device_step(): stats = lax.all_gather(jnp.stack([loc_mean, loc_m2]), 'dm', axis=0)]
    unnamed x22 -> x30, local copies, waits for them, and re-layouts: 46.7 us -> 48.3 us
  transfers between devices with their start and end apart: 3 -> 3, of which waited for: 3 -> 3; matrix products, arithmetic and copies ran while one was open for 8% -> 2% of each run, Pallas kernels for 0% -> 0%
where the time goes in v1:
time: 493 us; the launch traced here: 491 us
  Pallas kernels  172 us (35%)
  waiting for transfers between devices  164 us (33%)
  local copies, waits for them, and re-layouts  55.7 us (11%)
  matrix products  43.5 us (9%)
  other arithmetic  22.5 us (5%)
  blocking collectives  19 us (4%)
  between operations  14.2 us (3%)
    pallas_call x1, Pallas kernels, project(): pl.pallas_call(functools.partial(project_kernel, nx, ntile), out_shape=(j...  172 us
    all_gather x1, waiting for transfers between devices, device_step(): act_all = lax.all_gather(act, 'dm', axis=0, tiled=True)  64.4 us
    psum x1, waiting for transfers between devices, device_step(): out_sum = lax.psum(part_out.astype(jnp.bfloat16), 'tp')  61.2 us
    unnamed x30, local copies, waits for them, and re-layouts  48.3 us
    all_gather x1, waiting for transfers between devices, device_step(): attn_all = lax.all_gather(attn_loc, 'dm', axis=0, tiled=True)  37.5 us
    all_gather x1, blocking collectives, device_step(): stats = lax.all_gather(jnp.stack([loc_mean, loc_m2]), 'dm', axis=0)  19 us
    dot_general x1, matrix products, device_step(): jnp.dot(act_all, w_down, preferred_element_type=jnp.float32)  17.6 us
  transfers between devices with their start and end apart: 3, of which 3 were waited for; matrix products, arithmetic and copies ran while one was open for 2% of the time, Pallas kernels for 0%

profile of v1, /device:TPU:97, one launch (start us, length us, event | category | flops | bytes accessed | tf_op | source)
XLA Modules:
  0.0 491.4 jit_solution(10186109114480859402)
XLA Ops:
  7.3 0.6 multiply_power_fusion
  7.9 1.6 convert_element_type.77
  9.5 0.8 iota_compare_fusion
  10.2 2.2 convert_reduce_fusion
  12.4 1.0 fusion.1
  13.5 19.0 %all-gather.1 = f32[8,2,2048]{2,1,0:T(2,128)S(1)} all-gather(f32[1,2,2048]{2,1,0:T(2,128)S(1)} %maximum_bitcast_fusion), channel_id=2, replica_groups=mesh['dp'=1,'tp'=4,'dm'=8] {'dm'}, dimensions={0}, use_global_device_ids=true | all-gather | bytes 147456 | tf_op jit(solution)/shard_map/all_gather | solution.py:269
  32.5 0.2 slice_reduce_fusion.1
  32.6 0.6 convert_element_type.71
  33.2 1.0 copy.37.wk_ref
  34.2 1.0 copy.38.wv_ref
  35.3 2.9 fusion.4.x_ref
  38.2 172.1 %project.1 = (bf16[256,1280]{1,0:T(8,128)(2,1)}, bf16[256,320]{1,0:T(8,128)(2,1)}, bf16[256,320]{1,0:T(8,128)(2,1)}, bf16[256,3456]{1,0:T(8,128)(2,1)}) custom-call(bf16[2048,640]{1,0:T(8,128)(2,1)} %fusion.4.x_ref, bf16[640,1280]{1,0:T(8,128)(2,1)} %wq_ref.1, bf16[640,320]{1,0:T(8,128)(2,1)} %copy.37.wk_ref, bf16[640,320]{1,0:T(8,128)(2,1)} %copy.38.wv_ref, ...), custom_call_target="tpu_custom_call" | custom-call | tf_op jit(solution)/shard_map/project/pallas_call | solution.py:199
  210.3 1.1 copy.45
  211.4 0.2 reshape.178
  211.7 0.1 reshape.180
  211.9 0.4 multiply_cosine_fusion
  212.3 0.2 multiply_multiply_fusion.1
  212.5 0.4 subtract_convert_fusion.1
  213.0 0.4 pad_maximum_fusion.1
  213.4 0.4 copy.51
  213.9 0.2 copy.39
  214.1 0.8 reshape.175
  215.0 0.1 multiply_reduce_fusion
  215.3 0.5 copy.42
  215.8 0.8 multiply_multiply_fusion
  216.7 2.0 subtract_convert_fusion
  218.7 1.5 pad_maximum_fusion
  220.2 0.2 convert_element_type.78
  220.5 1.0 copy.43
  221.5 23.1 %copy.44 = bf16[256,2,64,160]{3,2,1,0:T(8,128)(2,1)} copy(bf16[256,2,64,160]{0,3,2,1:T(8,128)(2,1)} %param.16) | data formatting | bytes 20971520 | tf_op args[2]
  244.6 0.7 fusion.16
  245.3 8.3 %fusion.15 = (f32[256,2,4]{2,1,0:T(2,128)S(1)}, f32[256,2,4,64]{3,2,1,0:T(4,128)S(1)}) fusion(bf16[256,2,4,160]{3,2,1,0:T(4,128)(2,1)S(1)} %copy.43, bf16[256,2,64,160]{3,2,1,0:T(8,128)(2,1)} %copy.44, pred[256,64]{1,0:T(8,128)(4,1)S(1)} %iota_compare_fusion), kind=kOutput, calls=%fused_computation.49 | convolution fusion | flops 42334208 | bytes 11689984 | tf_op jit(solution)/shard_map/rkgd,rksd->rkgs/dot_general | solution.py:234
  253.7 0.2 multiply_maximum_fusion
  253.9 1.4 fusion.8
  255.3 1.1 fusion.14
  256.6 0.2 copy.49
  256.8 23.1 %copy.47 = bf16[256,2,64,160]{3,2,1,0:T(8,128)(2,1)} copy(bf16[256,2,64,160]{0,3,2,1:T(8,128)(2,1)} %param.17) | data formatting | bytes 20971520 | tf_op args[3]
  279.9 7.3 %fusion.6 = bf16[256,2,4,160]{3,2,1,0:T(4,128)(2,1)S(1)} fusion(bf16[256,2,64,160]{3,2,1,0:T(8,128)(2,1)} %copy.47, f32[256,2,4]{2,1,0:T(2,128)S(1)} %copy-done.6, f32[256,2,160]{2,1,0:T(2,128)S(1)} %copy.49, f32[256,2,4]{2,1,0:T(2,128)} %get-tuple-element.17, f32[256,2,4,64]{3,2,1,0:T(4,128)S(1)} %get-tuple-element.26, ...), kind=kOutput, calls=%fused_computation.12 | convolution fusion | flops 43515904 | bytes 12017664 | tf_op jit(solution)/shard_map/rkgs,rksd->rkgd/dot_general | solution.py:242
  287.2 1.5 copy.50
  288.8 0.7 all-gather.7.cloned.1.call-update
  289.5 0.3 all-reduce.2.cloned.1.call-start
  289.9 37.5 %all-gather.5.cloned.1.call-done = bf16[2048,1280]{0,1:T(8,128)(2,1)} async-done(((bf16[256,1280]{0,1:T(8,128)(2,1)}), bf16[2048,1280]{0,1:T(8,128)(2,1)}) %all-gather.5.cloned.1.call-update) | async-done | bytes 5242896 | tf_op jit(solution)/shard_map/all_gather | solution.py:282
  327.4 9.6 %fusion.17 = f32[2048,640]{1,0:T(8,128)} fusion(bf16[2048,1280]{0,1:T(8,128)(2,1)} %all-gather.5.cloned.1.call-done, bf16[1280,640]{1,0:T(8,128)(2,1)} %param.26), kind=kOutput, calls=%fused_computation.51 | convolution fusion | flops 3355443200 | bytes 12124160 | tf_op jit(solution)/shard_map/dot_general | solution.py:283
  337.0 64.4 %all-gather.7.cloned.1.call-done = bf16[2048,3456]{1,0:T(8,128)(2,1)} async-done(((bf16[256,3456]{1,0:T(8,128)(2,1)}), bf16[2048,3456]{1,0:T(8,128)(2,1)}) %all-gather.7.cloned.1.call-update) | async-done | bytes 14155792 | tf_op jit(solution)/shard_map/all_gather | solution.py:281
  401.4 17.6 %add_convert_fusion = bf16[2048,640]{1,0:T(8,128)(2,1)} fusion(f32[2048,640]{1,0:T(8,128)} %fusion.17, bf16[2048,3456]{1,0:T(8,128)(2,1)} %all-gather.7.cloned.1.call-done, bf16[3456,640]{1,0:T(8,128)(2,1)} %param.27), kind=kOutput, calls=%fused_computation.10 | convolution fusion | flops 9062318080 | bytes 26443776 | tf_op jit(solution)/shard_map/dot_general | solution.py:283
  419.1 0.7 convert_element_type.83
  419.8 61.2 %all-reduce.2.cloned.1.call-done = bf16[2048,640]{1,0:T(8,128)(2,1)} async-done(((bf16[2048,640]{1,0:T(8,128)(2,1)}), bf16[2048,640]{1,0:T(8,128)(2,1)}) %all-reduce.2.cloned.1.call-update) | async-done | bytes 2621456 | tf_op jit(solution)/shard_map/psum | solution.py:284
  481.0 3.9 fusion.5
  (45 shorter events, 0.9 us)
Async XLA Ops:
  7.2 5.2 %copy-start = (bf16[2048,640]{1,0:T(8,128)(2,1)S(1)}, bf16[2048,640]{1,0:T(8,128)(2,1)}, u32[]{:S(2)}) copy-start(bf16[2048,640]{1,0:T(8,128)(2,1)} %param.14) | copy-start | bytes 7864324
  7.2 26.1 %copy-start.4 = (bf16[640,320]{0,1:T(8,128)(2,1)S(1)}, bf16[640,320]{0,1:T(8,128)(2,1)}, u32[]{:S(2)}) copy-start(bf16[640,320]{0,1:T(8,128)(2,1)} %param.20) | copy-start | bytes 1228804
  7.2 27.0 %copy-start.5 = (bf16[640,320]{0,1:T(8,128)(2,1)S(1)}, bf16[640,320]{0,1:T(8,128)(2,1)}, u32[]{:S(2)}) copy-start(bf16[640,320]{0,1:T(8,128)(2,1)} %param.21) | copy-start | bytes 1228804
  7.2 320.2 %all-gather.5.cloned.1.call-start = ((), (), s32[]{:S(2)}) async-start(), calls=%async_computation | async-start | bytes 5898240 | tf_op jit(solution)/shard_map/all_gather | solution.py:282
  7.3 25.4 %copy-start.10 = (bf16[640]{0:T(1024)(128)(2,1)S(1)}, bf16[640]{0:T(1024)(128)(2,1)}, u32[]{:S(2)}) copy-start(bf16[640]{0:T(1024)(128)(2,1)} %param.18) | copy-start | bytes 3844
  38.2 173.5 %copy-start.11 = (bf16[2,160]{1,0:T(2,128)(2,1)S(1)}, bf16[2,160]{1,0:T(2,128)(2,1)}, u32[]{:S(2)}) copy-start(bf16[2,160]{1,0:T(2,128)(2,1)} %param.25) | copy-start | bytes 1924
  38.2 173.7 %copy-start.8 = (f32[256]{0:T(256)S(1)}, f32[256]{0:T(256)}, u32[]{:S(2)}) copy-start(f32[256]{0:T(256)} %convert_element_type.77) | copy-start | bytes 3076
  38.2 173.7 %copy-start.12 = (f32[80]{0:T(128)S(1)}, f32[80]{0:T(128)}, u32[]{:S(2)}) copy-start(f32[80]{0:T(128)} %multiply_power_fusion) | copy-start | bytes 964
  210.3 3.6 copy-start.3
  212.9 2.2 copy-start.9
  245.3 11.1 %copy-start.7 = (bf16[256,320]{1,0:T(8,128)(2,1)S(1)}, bf16[256,320]{1,0:T(8,128)(2,1)}, u32[]{:S(2)}) copy-start(bf16[256,320]{1,0:T(8,128)(2,1)} %get-tuple-element.9) | copy-start | bytes 491524
  256.6 23.3 %copy-start.2 = (bf16[256,320]{0,1:T(8,128)(2,1)}, bf16[256,320]{0,1:T(8,128)(2,1)S(1)}, u32[]{:S(2)}) copy-start(bf16[256,320]{0,1:T(8,128)(2,1)S(1)} %copy.48) | copy-start | bytes 491524
  256.8 23.2 %copy-start.6 = (f32[256,2,4]{2,1,0:T(2,128)S(1)}, f32[256,2,4]{2,1,0:T(2,128)}, u32[]{:S(2)}) copy-start(f32[256,2,4]{2,1,0:T(2,128)} %get-tuple-element.16) | copy-start | bytes 24580
  288.7 112.6 %all-gather.7.cloned.1.call-start = ((), (), s32[]{:S(2)}) async-start(), calls=%async_computation.1 | async-start | bytes 15925248 | tf_op jit(solution)/shard_map/all_gather | solution.py:281
  289.5 191.4 %all-reduce.2.cloned.1.call-start = ((), (), s32[]{:S(2)}) async-start(), calls=%async_computation.2 | async-start | bytes 5242880 | tf_op jit(solution)/shard_map/psum | solution.py:284
  419.0 62.0 %copy-start.1 = (bf16[2048,640]{1,0:T(8,128)(2,1)S(1)}, bf16[2048,640]{1,0:T(8,128)(2,1)}, u32[]{:S(2)}) copy-start(bf16[2048,640]{1,0:T(8,128)(2,1)} %param.14) | copy-start | bytes 7864324
Sparse Core Ops, SparseCore 0:
  288.9 38.4 all-gather.4
  329.0 72.3 all-gather.6
  419.2 61.7 all-reduce.1

commit v2 on v1

--- a/solution.py
+++ b/solution.py
@@ -16,27 +16,8 @@
 VMEM_LIMIT = 66 * 1024 * 1000 - 1024 * 600
 
 
-def layer_norm_last(values, gain_w):
-    centred = values - jnp.mean(values, axis=-1, keepdims=True)
-    spread = jnp.mean(centred * centred, axis=-1, keepdims=True)
-    return centred * lax.rsqrt(spread + NORM_EPS) * gain_w
-
-
-def rotary(values, positions):
-    head_dim = values.shape[-1]
-    inv_freq = ROPE_THETA ** (-jnp.arange(0, head_dim, 2, dtype=jnp.float32) / head_dim)
-    angles = positions.astype(jnp.float32)[:, None] * inv_freq[None, :]
-    cos_a = jnp.cos(angles)[:, None, :]
-    sin_a = jnp.sin(angles)[:, None, :]
-    pair_view = values.reshape(values.shape[:-1] + (head_dim // 2, 2))
-    even_part = pair_view[..., 0]
-    odd_part = pair_view[..., 1]
-    turned = jnp.stack([even_part * cos_a - odd_part * sin_a, odd_part * cos_a + even_part * sin_a], axis=-1)
-    return turned.reshape(values.shape)
-
-
 def project_kernel(nx, ntile, x_ref, wq_ref, wk_ref, wv_ref, wg_ref, wu_ref,
-                   q_out, k_out, v_out, act_out,
+                   qk_out, v_out, act_out,
                    xbuf, bq, bk, bv, bg, bu, rq, rk, rg, lq, lv, lu,
                    x_loc, x_snd, x_rcv, w_loc, w_snd, w_rcv, r_snd, r_rcv):
     dm = lax.axis_index('dm')
@@ -170,9 +151,10 @@
         return lax.fori_loop(0, ntile, mlp, carry)
 
     lax.fori_loop(0, nx, step, 0)
-    q_out[:, :half] = rq[nx - 1]
-    q_out[:, half:] = lq[nx - 1]
-    k_out[...] = rk[nx - 1]
+    qk_out[:, :half] = rq[nx - 1]
+    qk_out[:, half:2 * half] = lq[nx - 1]
+    qk_out[:, 2 * half:2 * half + kw] = rk[nx - 1]
+    qk_out[:, 2 * half + kw:] = jnp.zeros((rb, qk_out.shape[1] - 2 * half - kw), BF16)
     v_out[...] = lv[nx - 1]
 
     def sent(s, carry):
@@ -198,10 +180,10 @@
     vmem = pl.BlockSpec(memory_space=pltpu.VMEM)
     return pl.pallas_call(
         functools.partial(project_kernel, nx, ntile),
-        out_shape=(jax.ShapeDtypeStruct((rb, nq), BF16), jax.ShapeDtypeStruct((rb, nk), BF16),
+        out_shape=(jax.ShapeDtypeStruct((rb, nq + pl.cdiv(nk, 128) * 128), BF16),
                    jax.ShapeDtypeStruct((rb, nk), BF16), jax.ShapeDtypeStruct((rb, nf), BF16)),
         in_specs=[pl.BlockSpec(memory_space=ANY)] * 6,
-        out_specs=(vmem,) * 4,
+        out_specs=(vmem,) * 3,
         scratch_shapes=[
             pltpu.VMEM((nx, rb, 2 * hid), BF16),
             pltpu.VMEM((2 * hid, nq), BF16),
@@ -229,19 +211,309 @@
     )(h, w_q, w_k, w_v, w_gate, w_up)
 
 
-def attend(q_rot, k_rot, v_new, k_cache, v_cache, positions):
-    score_scale = q_rot.shape[-1] ** -0.5
-    s_cache = jnp.einsum('rkgd,rksd->rkgs', q_rot, k_cache, preferred_element_type=jnp.float32) * score_scale
-    key_valid = jnp.arange(k_cache.shape[2])[None, None, None, :] < positions[:, None, None, None]
-    s_cache = jnp.where(key_valid, s_cache, -1e30)
-    s_new = jnp.einsum('rkgd,rkd->rkg', q_rot, k_rot, preferred_element_type=jnp.float32) * score_scale
-    row_max = jnp.maximum(jnp.max(s_cache, axis=-1), s_new)
-    p_cache = jnp.exp(s_cache - row_max[..., None])
-    p_new = jnp.exp(s_new - row_max)
-    denom_sum = jnp.sum(p_cache, axis=-1) + p_new
-    numer_acc = jnp.einsum('rkgs,rksd->rkgd', p_cache.astype(jnp.bfloat16), v_cache, preferred_element_type=jnp.float32)
-    numer_acc = numer_acc + p_new[..., None] * v_new.astype(jnp.float32)[:, :, None, :]
-    return (numer_acc / denom_sum[..., None]).astype(jnp.bfloat16)
+def swap_pairs(v):
+    width = v.shape[-1]
+    lane = lax.broadcasted_iota(jnp.int32, v.shape, v.ndim - 1)
+    return jnp.where(lax.rem(lane, 2) == 0, pltpu.roll(v, width - 1, v.ndim - 1), pltpu.roll(v, 1, v.ndim - 1))
+
+
+def finish_kernel(nx, ny, heads, kv_heads, act_ref, qk_ref, v_ref, kc_ref, vc_ref, hi_ref, cos_ref, sin_ref, gain_ref, gswap_ref,
+                  wo_ref, wd_ref, x_ref, out_ref, k_out,
+                  gath, w2, qb, kbuf, vbuf, pb, r1, mf, mq, r2,
+                  c_loc, kv_loc, s_own, s_opp, s_par, recv, y1s, y1r, y2s, y2r, y3s, y3r, y4s, y4r):
+    dm = lax.axis_index('dm')
+    y = lax.axis_index('tp')
+    xi = dm // 2
+    core = lax.rem(dm, 2)
+    other = 2 * xi + 1 - core
+    right = lax.rem(xi + 1, nx) * 2 + core
+    left = lax.rem(xi + nx - 1, nx) * 2 + core
+    nf = act_ref.shape[1]
+    rb = act_ref.shape[0]
+    hb, qtr = rb // 2, rb // 4
+    head = cos_ref.shape[1]
+    natt = heads * head
+    group = heads // kv_heads
+    flip, mirror = y + 1 - 2 * lax.rem(y, 2), ny - 1 - y
+    p1 = flip + core * (mirror - flip)
+    p2 = mirror + core * (flip - mirror)
+    bit_a, bit_b, bit_c = lax.rem((y + 1) // 2, 2), y // 2, lax.rem(y, 2)
+    b1 = bit_a + core * (bit_b - bit_a)
+    b2 = bit_b + core * (bit_c - bit_b)
+
+    act_cols, att_cols = pl.ds(natt, nf), pl.ds(0, natt)
+
+    def to(peer):
+        return dict(device_id={'dm': peer}, device_id_type=MESH)
+
+    def to_y(peer):
+        return dict(device_id={'tp': peer}, device_id_type=MESH)
+
+    def own_send(n, h, kind):
+        peer, slot = ((right, 4), (left, 2), (other, 1))[n]
+        cols = att_cols if kind else act_cols
+        src = gath.at[0, pl.ds(h * hb, hb), cols] if kind else act_ref.at[pl.ds(h * hb, hb), :]
+        return pltpu.make_async_remote_copy(
+            src_ref=src, dst_ref=gath.at[slot, pl.ds(h * hb, hb), cols],
+            send_sem=s_own.at[n, h, kind], recv_sem=recv.at[slot, h, kind], **to(peer))
+
+    def opp_send(n, kind):
+        peer, slot, h = ((right, 4, 0), (left, 2, 1))[n]
+        cols = att_cols if kind else act_cols
+        return pltpu.make_async_remote_copy(
+            src_ref=gath.at[slot, pl.ds(h * hb, hb), cols], dst_ref=gath.at[6, pl.ds(h * hb, hb), cols],
+            send_sem=s_opp.at[n, kind], recv_sem=recv.at[6, h, kind], **to(peer))
+
+    def par_send(slot, h, kind):
+        cols = att_cols if kind else act_cols
+        return pltpu.make_async_remote_copy(
+            src_ref=gath.at[slot, pl.ds(h * hb, hb), cols], dst_ref=gath.at[slot + 1, pl.ds(h * hb, hb), cols],
+            send_sem=s_par.at[slot // 2 - 1, h, kind], recv_sem=recv.at[slot + 1, h, kind], **to(other))
+
+    def landed(slot, h, kind):
+        cols = att_cols if kind else act_cols
+        part = gath.at[slot, pl.ds(h * hb, hb), cols]
+        return pltpu.make_async_remote_copy(
+            src_ref=part, dst_ref=part, send_sem=s_own.at[0, 0, 0], recv_sem=recv.at[slot, h, kind], **to(other))
+
+    n_loc = 3
+    locals_ = [pltpu.make_async_copy(act_ref, gath.at[0, :, act_cols], c_loc.at[0]),
+               pltpu.make_async_copy(wo_ref, w2.at[att_cols, :], c_loc.at[1]),
+               pltpu.make_async_copy(wd_ref, w2.at[act_cols, :], c_loc.at[2])]
+
+    rg = kbuf.shape[1]
+    n_groups = rb // rg
+
+    def cache_copies(g, slot):
+        rows = pl.ds(g * rg, rg)
+        return (pltpu.make_async_copy(kc_ref.at[rows], kbuf.at[slot], kv_loc.at[0, slot]),
+                pltpu.make_async_copy(vc_ref.at[rows], vbuf.at[slot], kv_loc.at[1, slot]))
+
+    for copy in cache_copies(0, 0):
+        copy.start()
+
+    barrier = pltpu.get_barrier_semaphore()
+    for peer in (other, right, left):
+        pl.semaphore_signal(barrier, inc=1, **to(peer))
+    for peer in (p1, p2):
+        pl.semaphore_signal(barrier, inc=1, **to_y(peer))
+    pl.semaphore_wait(barrier, 5)
+
+    for h in range(2):
+        for n in range(3):
+            own_send(n, h, 0).start()
+    for copy in locals_:
+        copy.start()
+
+    qk = qk_ref[...].astype(F32)
+    qk_swap = swap_pairs(qk)
+    cos_a, sin_a = cos_ref[...], sin_ref[...]
+    for n in range(heads + kv_heads):
+        one = qk[:, n * head:(n + 1) * head]
+        two = qk_swap[:, n * head:(n + 1) * head]
+        mean = jnp.mean(one, axis=-1, keepdims=True)
+        centred = one - mean
+        scale = lax.rsqrt(jnp.mean(centred * centred, axis=-1, keepdims=True) + NORM_EPS)
+        turned = centred * scale * gain_ref[n:n + 1, :] * cos_a + (two - mean) * scale * gswap_ref[n:n + 1, :] * sin_a
+        qb[n] = turned.astype(BF16)
+        if n >= heads:
+            k_out[n - heads] = turned.astype(BF16)
+
+    ctx = kbuf.shape[3]
+    score_scale = head ** -0.5
+    wide = group * rg
+    nt = (((1,), (1,)), ((), ()))
+    tn = (((0,), (0,)), ((), ()))
+
+    def attend_group(g, carry):
+        slot = lax.rem(g, 2)
+        for copy in cache_copies(g, slot):
+            copy.wait()
+
+        @pl.when(g < n_groups - 1)
+        def _():
+            for copy in cache_copies(g + 1, 1 - slot):
+                copy.start()
+
+        rows = pl.ds(pl.multiple_of(g * rg, rg), rg)
+        col_row = lax.rem(lax.broadcasted_iota(jnp.int32, (1, wide), 1), rg)
+        low = col_row * ctx
+        high = hi_ref[g]
+        for kv in range(kv_heads):
+            q_cols = jnp.concatenate([qb[kv * group + j, rows, :] for j in range(group)], axis=0)
+            keys = kbuf[slot, :, kv].reshape(rg * ctx, head)
+            vals = vbuf[slot, :, kv].reshape(rg * ctx, head)
+            k_one = qb[heads + kv, rows, :]
+            v_one = v_ref[rows, kv * head:(kv + 1) * head]
+            scores = lax.dot_general(keys, q_cols, nt, preferred_element_type=F32) * score_scale
+            at = lax.broadcasted_iota(jnp.int32, scores.shape, 0)
+            scores = jnp.where((at >= low) & (at < high), scores, -1e30)
+            s_one = lax.dot_general(k_one, q_cols, nt, preferred_element_type=F32) * score_scale
+            at_one = lax.broadcasted_iota(jnp.int32, s_one.shape, 0)
+            s_one = jnp.where(at_one == col_row, s_one, -1e30)
+            top = jnp.maximum(jnp.max(scores, axis=0, keepdims=True), jnp.max(s_one, axis=0, keepdims=True))
+            probs = jnp.exp(scores - top)
+            p_one = jnp.exp(s_one - top)
+            denom = jnp.sum(probs, axis=0, keepdims=True) + jnp.sum(p_one, axis=0, keepdims=True)
+            p_high = p_one.astype(BF16)
+            p_low = (p_one - p_high.astype(F32)).astype(BF16)
+            numer = lax.dot_general(probs.astype(BF16), vals, tn, preferred_element_type=F32)
+            numer = numer + lax.dot_general(p_high, v_one, tn, preferred_element_type=F32)
+            numer = numer + lax.dot_general(p_low, v_one, tn, preferred_element_type=F32)
+            denom_col = jnp.transpose(jnp.broadcast_to(denom, (wide, wide)))[:, 0:1]
+            result = (numer / denom_col).astype(BF16)
+            for j in range(group):
+                n = kv * group + j
+                gath[0, rows, n * head:(n + 1) * head] = result[j * rg:(j + 1) * rg]
+        return carry
+
+    lax.fori_loop(0, n_groups, attend_group, 0)
+    for h in range(2):
+        for n in range(3):
+            own_send(n, h, 1).start()
+    for copy in locals_:
+        copy.wait()
+
+    def block_rows(place, j):
+        off = place + (place // 2) * (5 - 2 * place)
+        who = core + j * (1 - 2 * core)
+        return (lax.rem(xi + off, nx) * 2 + who) * rb
+
+    def y1(i):
+        return pltpu.make_async_remote_copy(
+            src_ref=pb.at[i, pl.ds(pl.multiple_of((1 - b1) * hb, hb), hb), :], dst_ref=r1.at[i],
+            send_sem=y1s.at[i], recv_sem=y1r.at[i], **to_y(p1))
+
+    def y2(i):
+        return pltpu.make_async_remote_copy(
+            src_ref=mq.at[i], dst_ref=r2.at[i], send_sem=y2s.at[i], recv_sem=y2r.at[i], **to_y(p2))
+
+    def y3(i, base, mine):
+        quarter = b2 if mine else 1 - b2
+        rows = out_ref.at[pl.ds(pl.multiple_of(base + b1 * hb + quarter * qtr, qtr), qtr), :]
+        return pltpu.make_async_remote_copy(
+            src_ref=rows, dst_ref=rows, send_sem=y3s.at[i], recv_sem=y3r.at[i], **to_y(p2))
+
+    def y4(i, base, mine):
+        half = b1 if mine else 1 - b1
+        rows = out_ref.at[pl.ds(pl.multiple_of(base + half * hb, hb), hb), :]
+        return pltpu.make_async_remote_copy(
+            src_ref=rows, dst_ref=rows, send_sem=y4s.at[i], recv_sem=y4r.at[i], **to_y(p1))
+
+    for place in range(nx):
+        if place == 1:
+            for kind in range(2):
+                for slot in (2, 4):
+                    for h in range(2):
+                        landed(slot, h, kind).wait_recv()
+                for n in range(2):
+                    opp_send(n, kind).start()
+                for slot in (2, 4):
+                    for h in range(2):
+                        par_send(slot, h, kind).start()
+        if place == 3:
+            for kind in range(2):
+                for h in range(2):
+                    landed(6, h, kind).wait_recv()
+                    par_send(6, h, kind).start()
+
+        def product(j, carry, place=place):
+            i = 2 * place + j
+
+            @pl.when(j == 1)
+            def _():
+                for kind in range(2):
+                    for h in range(2):
+                        landed(2 * place + 1, h, kind).wait_recv()
+
+            part = jnp.dot(gath[i], w2[...], preferred_element_type=F32)
+            pb[i] = part.astype(BF16)
+            mf[j] = part
+            y1(i).start()
+            return carry
+
+        lax.fori_loop(0, 2, product, 0)
+        for j in range(2):
+            i = 2 * place + j
+            y1(i).wait_recv()
+            send_rows = pl.ds(pl.multiple_of(b1 * hb + (1 - b2) * qtr, qtr), qtr)
+            send_sub = pl.ds(pl.multiple_of((1 - b2) * qtr, qtr), qtr)
+            mq[i] = (mf[j, send_rows, :] + r1[i, send_sub, :].astype(F32)).astype(BF16)
+            y2(i).start()
+        for j in range(2):
+            i = 2 * place + j
+            y2(i).wait_recv()
+            base = block_rows(place, j)
+            keep_rows = pl.ds(pl.multiple_of(b1 * hb + b2 * qtr, qtr), qtr)
+            keep_sub = pl.ds(pl.multiple_of(b2 * qtr, qtr), qtr)
+            total = mf[j, keep_rows, :] + r1[i, keep_sub, :].astype(F32) + r2[i].astype(F32)
+            rows = pl.ds(pl.multiple_of(base + b1 * hb + b2 * qtr, qtr), qtr)
+            out_ref[rows, :] = (x_ref[rows, :].astype(F32) + total).astype(BF16)
+            y3(i, base, True).start()
+        for j in range(2):
+            i = 2 * place + j
+            base = block_rows(place, j)
+            y3(i, base, False).wait_recv()
+            y4(i, base, True).start()
+
+    for place in range(nx):
+        for j in range(2):
+            i = 2 * place + j
+            base = block_rows(place, j)
+            y4(i, base, False).wait_recv()
+            y1(i).wait_send()
+            y2(i).wait_send()
+            y3(i, base, True).wait_send()
+            y4(i, base, True).wait_send()
+    for kind in range(2):
+        for h in range(2):
+            for n in range(3):
+                own_send(n, h, kind).wait_send()
+            for slot in (2, 4, 6):
+                par_send(slot, h, kind).wait_send()
+        for n in range(2):
+            opp_send(n, kind).wait_send()
+
+
+def finish(nx, ny, act, qk, v_rows, k_cache, v_cache, positions, cos_a, sin_a, gains, gains_swap, w_out, w_down, x_in):
+    rb, nf = act.shape
+    kv_heads, ctx, head = k_cache.shape[1:]
+    natt, wcols = w_out.shape
+    heads = natt // head
+    group = heads // kv_heads
+    rg = 128 // group
+    wide = group * rg
+    col = jnp.arange(wide) % rg
+    high = (positions.reshape(rb // rg, rg)[:, col] + ctx * col[None, :]).astype(jnp.int32)[:, None, :]
+    vmem = pl.BlockSpec(memory_space=pltpu.VMEM)
+    hbm = pl.BlockSpec(memory_space=ANY)
+    dma = pltpu.SemaphoreType.DMA
+    return pl.pallas_call(
+        functools.partial(finish_kernel, nx, ny, heads, kv_heads),
+        out_shape=(jax.ShapeDtypeStruct(x_in.shape, BF16), jax.ShapeDtypeStruct((kv_heads, rb, head), BF16)),
+        in_specs=[hbm, vmem, vmem, hbm, hbm, vmem, vmem, vmem, vmem, vmem, hbm, hbm, vmem],
+        out_specs=(vmem, vmem),
+        scratch_shapes=[
+            pltpu.VMEM((2 * nx, rb, natt + nf), BF16),
+            pltpu.VMEM((natt + nf, wcols), BF16),
+            pltpu.VMEM((heads + kv_heads, rb, head), BF16),
+            pltpu.VMEM((2, rg, kv_heads, ctx, head), BF16),
+            pltpu.VMEM((2, rg, kv_heads, ctx, head), BF16),
+            pltpu.VMEM((2 * nx, rb, wcols), BF16),
+            pltpu.VMEM((2 * nx, rb // 2, wcols), BF16),
+            pltpu.VMEM((2, rb, wcols), F32),
+            pltpu.VMEM((2 * nx, rb // 4, wcols), BF16),
+            pltpu.VMEM((2 * nx, rb // 4, wcols), BF16),
+            dma((3,)),
+            dma((2, 2)),
+            dma((3, 2, 2)),
+            dma((2, 2)),
+            dma((3, 2, 2)),
+            dma((2 * nx, 2, 2)),
+        ] + [dma((2 * nx,))] * 8,
+        compiler_params=pltpu.CompilerParams(collective_id=1, has_side_effects=True, vmem_limit_bytes=VMEM_LIMIT),
+        name='finish',
+    )(act, qk, v_rows, k_cache, v_cache, high, cos_a, sin_a, gains, gains_swap, w_out, w_down, x_in)
 
 
 def solution(mesh):
@@ -259,7 +531,6 @@
         rows_loc = k_cache.shape[0]
         kv_loc = k_cache.shape[1]
         head_dim = k_cache.shape[3]
-        heads_loc = q_gain.shape[0]
         hid = x_in.shape[1]
         d_model = hid * dm_size
         x_f32 = x_in.astype(jnp.float32)
@@ -271,18 +542,17 @@
         diff = stats[:, 0] - row_mean[None]
         row_var = (jnp.sum(stats[:, 1], axis=0) + hid * jnp.sum(diff * diff, axis=0)) / d_model
         normed = ((x_f32 - row_mean[:, None]) * lax.rsqrt(row_var + NORM_EPS)[:, None] * ln_gain.astype(jnp.float32)).astype(jnp.bfloat16)
-        q_rows, k_rows, v_rows, act = project(nx, normed, w_q, w_k, w_v, w_gate, w_up)
-        q_heads = layer_norm_last(q_rows.reshape(rows_loc, heads_loc, head_dim).astype(jnp.float32), q_gain.astype(jnp.float32))
-        q_rot = rotary(q_heads, positions).astype(jnp.bfloat16).reshape(rows_loc, kv_loc, heads_loc // kv_loc, head_dim)
-        k_heads = layer_norm_last(k_rows.reshape(rows_loc, kv_loc, head_dim).astype(jnp.float32), k_gain.astype(jnp.float32))
-        k_new = rotary(k_heads, positions).astype(jnp.bfloat16)
+        qk, v_rows, act = project(nx, normed, w_q, w_k, w_v, w_gate, w_up)
+        inv_freq = ROPE_THETA ** (-(jnp.arange(head_dim) // 2 * 2).astype(jnp.float32) / head_dim)
+        angles = positions.astype(jnp.float32)[:, None] * inv_freq[None, :]
+        odd = jnp.arange(head_dim) % 2
+        sin_a = jnp.sin(angles) * (2 * odd - 1).astype(jnp.float32)[None, :]
+        gains = jnp.concatenate([q_gain, k_gain], axis=0).astype(jnp.float32)
+        gains_swap = gains.reshape(-1, head_dim // 2, 2)[:, :, ::-1].reshape(gains.shape)
+        x_out, k_heads = finish(nx, mesh.shape['tp'], act, qk, v_rows, k_cache, v_cache, positions, jnp.cos(angles), sin_a,
+                                gains, gains_swap, w_out, w_down, x_in)
+        k_new = jnp.transpose(k_heads, (1, 0, 2))
         v_new = v_rows.reshape(rows_loc, kv_loc, head_dim)
-        attn_loc = attend(q_rot, k_new, v_new, k_cache, v_cache, positions).reshape(rows_loc, heads_loc * head_dim)
-        act_all = lax.all_gather(act, 'dm', axis=0, tiled=True)
-        attn_all = lax.all_gather(attn_loc, 'dm', axis=0, tiled=True)
-        part_out = jnp.dot(attn_all, w_out, preferred_element_type=jnp.float32) + jnp.dot(act_all, w_down, preferred_element_type=jnp.float32)
-        out_sum = lax.psum(part_out.astype(jnp.bfloat16), 'tp')
-        x_out = (x_f32 + out_sum.astype(jnp.float32)).astype(jnp.bfloat16)
         return x_out, k_new, v_new
 
     return jax.shard_map(

time: 493 us -> 384 us (0.78)
  waiting for transfers between devices: 164 us -> 0 us
  Pallas kernels: 172 us -> 296 us
  matrix products: 43.5 us -> 0 us
  between operations: 14.2 us -> 0.81 us
  other arithmetic: 22.5 us -> 10.4 us
    pallas_call x0 -> x1, Pallas kernels: none -> 124 us  [finish(): pl.pallas_call(functools.partial(finish_kernel, nx, ny, heads, kv_heads),...]
    all_gather x2 -> x0, waiting for transfers between devices: 102 us -> none  [the longest x1 64.4 us: device_step(): act_all = lax.all_gather(act, 'dm', axis=0, tiled=True)]
    psum x1 -> x0, waiting for transfers between devices: 61.2 us -> none  [device_step(): out_sum = lax.psum(part_out.astype(jnp.bfloat16), 'tp')]
    dot_general x5 -> x0, matrix products: 43.5 us -> none  [the longest x1 17.6 us: device_step(): jnp.dot(act_all, w_down, preferred_element_type=jnp.float32)]
    convert_element_type x11 -> x0, local copies, waits for them, and re-layouts: 6.49 us -> none  [the longest x1 1.5 us: attend(): return (numer_acc / denom_sum[..., None]).astype(jnp.bfloat16)]
    unnamed x30 -> x21, local copies, waits for them, and re-layouts: 48.3 us -> 53.3 us
  transfers between devices with their start and end apart: 3 -> 0, of which waited for: 3 -> 0; matrix products, arithmetic and copies ran while one was open for 2% -> 0% of each run, Pallas kernels for 0% -> 0%
where the time goes in v2:
time: 384 us; the launch traced here: 383 us
  Pallas kernels  296 us (77%)
  local copies, waits for them, and re-layouts  57 us (15%)
  blocking collectives  19 us (5%)
  other arithmetic  10.4 us (3%)
    pallas_call x1, Pallas kernels, project(): pl.pallas_call(functools.partial(project_kernel, nx, ntile), out_shape=(j...  172 us
    pallas_call x1, Pallas kernels, finish(): pl.pallas_call(functools.partial(finish_kernel, nx, ny, heads, kv_heads),...  124 us
    unnamed x21, local copies, waits for them, and re-layouts  53.3 us
    all_gather x1, blocking collectives, device_step(): stats = lax.all_gather(jnp.stack([loc_mean, loc_m2]), 'dm', axis=0)  19 us

profile of v2, /device:TPU:97, one launch (start us, length us, event | category | flops | bytes accessed | tf_op | source)
XLA Modules:
  0.0 383.1 jit_solution(18104898646942023365)
XLA Ops:
  0.6 0.0 copy-start
  0.6 0.0 copy-start.6
  0.7 0.0 copy-start.1
  0.7 2.3 convert_reduce_fusion
  3.0 0.0 copy-start.2
  3.0 2.7 fusion.1
  5.8 19.0 %all-gather.1 = f32[8,2,2048]{2,1,0:T(2,128)S(1)} all-gather(f32[1,2,2048]{2,1,0:T(2,128)S(1)} %maximum_bitcast_fusion), channel_id=2, replica_groups=mesh['dp'=1,'tp'=4,'dm'=8] {'dm'}, dimensions={0}, use_global_device_ids=true | all-gather | bytes 147456 | tf_op jit(solution)/shard_map/all_gather | solution.py:540
  24.8 0.2 slice_reduce_fusion.1
  25.0 0.0 copy-done.6
  25.0 0.0 copy-done
  25.1 2.0 fusion.4.x_ref
  27.1 0.0 copy-done.1
  27.1 1.0 copy.35.wk_ref
  28.1 0.0 copy-done.2
  28.1 1.0 copy.36.wv_ref
  29.1 0.0 copy-start.4
  29.1 172.0 %project.1 = (bf16[256,1664]{1,0:T(8,128)(2,1)}, bf16[256,320]{1,0:T(8,128)(2,1)}, bf16[256,3456]{1,0:T(8,128)(2,1)}) custom-call(bf16[2048,640]{1,0:T(8,128)(2,1)} %fusion.4.x_ref, bf16[640,1280]{1,0:T(8,128)(2,1)} %wq_ref.1, bf16[640,320]{1,0:T(8,128)(2,1)} %copy.35.wk_ref, bf16[640,320]{1,0:T(8,128)(2,1)} %copy.36.wv_ref, bf16[640,3456]{1,0:T(8,128)(2,1)} %wg_ref.1, ...), custom_call_target="tpu_custom_call" | custom-call | tf_op jit(solution)/shard_map/project/pallas_call | solution.py:181
  201.1 0.0 copy-done.4
  201.1 1.8 fusion.5
  203.0 23.1 %copy.43.kc_ref = bf16[256,2,64,160]{3,2,1,0:T(8,128)(2,1)} copy(bf16[256,2,64,160]{0,3,2,1:T(8,128)(2,1)} %param.16) | data formatting | bytes 20971520 | tf_op args[2]
  226.0 0.0 copy-start.3
  226.0 0.0 copy-start.5
  226.0 22.8 %copy.44.vc_ref = bf16[256,2,64,160]{3,2,1,0:T(8,128)(2,1)} copy(bf16[256,2,64,160]{0,3,2,1:T(8,128)(2,1)} %param.17) | data formatting | bytes 20971520 | tf_op args[3]
  248.9 0.0 copy-done.3
  248.9 0.1 copy.39
  249.0 0.1 copy.40
  249.1 0.0 copy-done.5
  249.1 0.2 concatenate.12
  249.3 0.1 copy.41
  249.4 0.1 copy.42
  249.5 0.7 copy.45.gswap_ref
  250.2 0.1 reshape.144
  250.3 0.1 copy.37
  250.4 0.6 gather_fusion
  251.1 0.6 broadcast_add_fusion.hi_ref
  251.7 0.6 maximum_convert_fusion.gain_ref
  252.3 123.8 %finish.1 = (bf16[2048,640]{1,0:T(8,128)(2,1)}, bf16[2,256,160]{2,1,0:T(8,128)(2,1)}) custom-call(bf16[256,3456]{1,0:T(8,128)(2,1)} %get-tuple-element.8.act_ref, bf16[256,1664]{1,0:T(8,128)(2,1)} %get-tuple-element.9.qk_ref, bf16[256,320]{1,0:T(8,128)(2,1)} %get-tuple-element.10.v_ref, bf16[256,2,64,160]{3,2,1,0:T(8,128)(2,1)} %copy.43.kc_ref, ...), custom_call_target="tpu_custom_call" | custom-call | tf_op jit(solution)/shard_map/finish/pallas_call | solution.py:491
  376.2 1.8 copy.47
  377.9 1.7 copy.46
  379.6 3.5 copy.51
  (15 shorter events, 0.2 us)
Async XLA Ops:
  0.6 24.4 %copy-start = (bf16[2048,640]{1,0:T(8,128)(2,1)S(1)}, bf16[2048,640]{1,0:T(8,128)(2,1)}, u32[]{:S(2)}) copy-start(bf16[2048,640]{1,0:T(8,128)(2,1)} %x_ref.1) | copy-start | bytes 7864324
  0.6 24.4 %copy-start.6 = (bf16[640]{0:T(1024)(128)(2,1)S(1)}, bf16[640]{0:T(1024)(128)(2,1)}, u32[]{:S(2)}) copy-start(bf16[640]{0:T(1024)(128)(2,1)} %param.18) | copy-start | bytes 3844
  0.7 26.4 %copy-start.1 = (bf16[640,320]{0,1:T(8,128)(2,1)S(1)}, bf16[640,320]{0,1:T(8,128)(2,1)}, u32[]{:S(2)}) copy-start(bf16[640,320]{0,1:T(8,128)(2,1)} %param.20) | copy-start | bytes 1228804
  3.0 25.1 %copy-start.2 = (bf16[640,320]{0,1:T(8,128)(2,1)S(1)}, bf16[640,320]{0,1:T(8,128)(2,1)}, u32[]{:S(2)}) copy-start(bf16[640,320]{0,1:T(8,128)(2,1)} %param.21) | copy-start | bytes 1228804
  29.1 172.0 %copy-start.4 = (s32[256]{0:T(256)S(1)}, s32[256]{0:T(256)}, u32[]{:S(2)}) copy-start(s32[256]{0:T(256)} %param.15) | copy-start | bytes 3076
  226.0 22.8 %copy-start.3 = (bf16[8,160]{1,0:T(8,128)(2,1)S(1)}, bf16[8,160]{1,0:T(8,128)(2,1)}, u32[]{:S(2)}) copy-start(bf16[8,160]{1,0:T(8,128)(2,1)} %param.24) | copy-start | bytes 7684
  226.0 23.0 %copy-start.5 = (bf16[2,160]{1,0:T(2,128)(2,1)S(1)}, bf16[2,160]{1,0:T(2,128)(2,1)}, u32[]{:S(2)}) copy-start(bf16[2,160]{1,0:T(2,128)(2,1)} %param.25) | copy-start | bytes 1924

commit v3 on v1

v3 whole, which is shorter than its diff:
```python
import functools
import math

import jax
import jax.numpy as jnp
from jax import lax
from jax.experimental import pallas as pl
from jax.experimental.pallas import tpu as pltpu
from jax.sharding import PartitionSpec as P

NORM_EPS = 1e-5
ROPE_THETA = 75000000.0
MESH = pl.DeviceIdType.MESH
BF16 = jnp.bfloat16
F32 = jnp.float32
ANY = pl.ANY
VMEM_LIMIT = 66 * 1024 * 1000 - 1024 * 600


def project_kernel(nx, ntile, x_ref, gain_ref, wq_ref, wk_ref, wv_ref, wg_ref, wu_ref,
                   qkv_out, act_out,
                   xbuf, gain, stat, bq, bkv, bg, bu, rq, rkv, rg, lq, lkv, lu,
                   x_loc, x_snd, x_rcv, t_snd, t_rcv, w_loc, w_snd, w_rcv, r_snd, r_rcv):
    dm = lax.axis_index('dm')
    xi = dm // 2
    core = lax.rem(dm, 2)
    other = 2 * xi + 1 - core
    right = lax.rem(xi + 1, nx) * 2 + core
    left = lax.rem(xi + nx - 1, nx) * 2 + core
    rb = xbuf.shape[1]
    hb = rb // 2
    hid = x_ref.shape[1]
    tw = wg_ref.shape[1] // ntile

    every = slice(None)
    kw = wk_ref.shape[0]
    pieces = [(wq_ref, bq, 0, every), (wk_ref, bkv, 1, pl.ds(0, kw)), (wv_ref, bkv, 1, pl.ds(kw, kw))]
    for t in range(ntile):
        pieces.append((wg_ref, bg, 0, pl.ds(t * tw, tw)))
        pieces.append((wu_ref, bu, 0, pl.ds(t * tw, tw)))

    def x_local(j):
        return pltpu.make_async_copy(
            x_ref.at[pl.ds((2 * j + core) * rb, rb), :], xbuf.at[j, :, pl.ds(0, hid)], x_loc.at[j])

    def x_remote(j):
        return pltpu.make_async_remote_copy(
            src_ref=x_ref.at[pl.ds((2 * j + 1 - core) * rb, rb), :], dst_ref=xbuf.at[j, :, pl.ds(hid, hid)],
            send_sem=x_snd.at[j], recv_sem=x_rcv.at[j], device_id={'dm': other}, device_id_type=MESH)

    def w_place(n, start):
        _, dst, side, cut = pieces[n]
        return dst.at[cut, pl.ds(start, hid)] if side else dst.at[pl.ds(start, hid), cut]

    def w_source(n):
        src, _, side, cut = pieces[n]
        return src if side else src.at[:, cut]

    def w_local(n):
        return pltpu.make_async_copy(w_source(n), w_place(n, 0), w_loc.at[n])

    def w_remote(n):
        return pltpu.make_async_remote_copy(
            src_ref=w_source(n), dst_ref=w_place(n, hid), send_sem=w_snd.at[n], recv_sem=w_rcv.at[n],
            device_id={'dm': other}, device_id_type=MESH)

    def g_remote():
        return pltpu.make_async_remote_copy(
            src_ref=gain.at[:, pl.ds(0, hid)], dst_ref=gain.at[:, pl.ds(hid, hid)], send_sem=x_snd.at[nx], recv_sem=x_rcv.at[nx],
            device_id={'dm': other}, device_id_type=MESH)

    def t_remote(d):
        return pltpu.make_async_remote_copy(
            src_ref=stat.at[0], dst_ref=stat.at[d], send_sem=t_snd.at[d - 1], recv_sem=t_rcv.at[d - 1],
            device_id={'dm': lax.rem(xi + d, nx) * 2 + core}, device_id_type=MESH)

    gain[:, 0:hid] = jnp.broadcast_to(gain_ref[...].astype(F32), (8, hid))
    for j in range(nx):
        x_local(j).start()
    for n in range(len(pieces)):
        w_local(n).start()

    barrier = pltpu.get_barrier_semaphore()
    pl.semaphore_signal(barrier, inc=1, device_id={'dm': other}, device_id_type=MESH)
    for d in range(1, nx):
        pl.semaphore_signal(barrier, inc=1, device_id={'dm': lax.rem(xi + d, nx) * 2 + core}, device_id_type=MESH)
    pl.semaphore_wait(barrier, nx)

    for j in range(nx):
        x_remote(j).start()
    g_remote().start()
    for n in range(3):
        w_remote(n).start()

    for ref in (rq, rkv, rg, lq, lkv, lu):
        ref[0] = jnp.zeros(ref.shape[1:], ref.dtype)

    lane = lax.broadcasted_iota(jnp.int32, (rb, 128), 1)
    both = jnp.zeros((rb, 128), F32)
    for j in range(nx):
        x_local(j).wait()
        x_remote(j).wait()
        values = xbuf[j].astype(F32)
        mean = jnp.mean(values, axis=1, keepdims=True)
        centred = values - mean
        both = jnp.where(lane == 2 * j, mean, both)
        both = jnp.where(lane == 2 * j + 1, jnp.sum(centred * centred, axis=1, keepdims=True), both)
    for n in range(3, 5):
        w_remote(n).start()
    stat[0] = jnp.transpose(both)[:2 * nx]
    for d in range(1, nx):
        t_remote(d).start()
    g_remote().wait()
    for d in range(1, nx):
        t_remote(d).wait()
    parts = [stat[d] for d in range(nx)]
    total = sum(parts[1:], parts[0])
    row_mean = total / nx
    spread = sum([(p - row_mean) * (p - row_mean) for p in parts[1:]], (parts[0] - row_mean) * (parts[0] - row_mean))
    variance = (total + 2 * hid * pltpu.roll(spread, 1, 0)) / (2 * hid * nx)
    line = lax.broadcasted_iota(jnp.int32, total.shape, 0)
    both = jnp.where(lax.rem(line, 2) == 0, row_mean, lax.rsqrt(variance + NORM_EPS))
    both = jnp.transpose(jnp.concatenate([both, jnp.zeros((128 - 2 * nx, rb), F32)], axis=0))
    for j in range(nx):
        values = xbuf[j].astype(F32) - both[:, 2 * j:2 * j + 1]
        xbuf[j] = (values * both[:, 2 * j + 1:2 * j + 2] * gain[0:1, :]).astype(BF16)

    def hop(d, t, s, slot, cols):
        nxt = jnp.minimum(s + 1, nx - 1)
        return pltpu.make_async_remote_copy(
            src_ref=slot.at[s, :, cols], dst_ref=slot.at[nxt, :, cols],
            send_sem=r_snd.at[d, t, s], recv_sem=r_rcv.at[d, t, nxt],
            device_id={'dm': left if d else right}, device_id_type=MESH)

    def arrived(d, t, s, slot, cols):
        return pltpu.make_async_remote_copy(
            src_ref=slot.at[s, :, cols], dst_ref=slot.at[s, :, cols],
            send_sem=r_snd.at[d, t, s], recv_sem=r_rcv.at[d, t, s],
            device_id={'dm': left if d else right}, device_id_type=MESH)

    def partial(d, s, weight, w_cols):
        row = lax.rem(xi + 1 + s, nx) if d else lax.rem(xi + 2 * nx - 1 - s, nx)
        if w_cols is None:
            return lax.dot_general(xbuf[row, d * hb:(d + 1) * hb, :], weight[...], (((1,), (1,)), ((), ())),
                                   preferred_element_type=F32)
        return jnp.dot(xbuf[row], weight[:, w_cols], preferred_element_type=F32)

    def pass_on(part, d, t, s, slot, cols):
        @pl.when(s > 0)
        def _():
            arrived(d, t, s, slot, cols).wait_recv()

        slot[s, :, cols] = (part + slot[s, :, cols].astype(F32)).astype(BF16)

        @pl.when(s < nx - 1)
        def _():
            hop(d, t, s, slot, cols).start()

    def wait_piece(n):
        w_local(n).wait()
        w_remote(n).wait()

    half = rq.shape[2]

    def step(s, carry):
        @pl.when(s == 0)
        def _():
            wait_piece(0)
            for n in range(5, len(pieces)):
                if (n - 3) // 2 == 1:
                    w_remote(n).start()

        pass_on(partial(0, s, bq, pl.ds(0, half)), 0, 0, s, rq, pl.ds(0, half))
        pass_on(partial(1, s, bq, pl.ds(half, half)), 1, 0, s, lq, pl.ds(0, half))

        @pl.when(s == 0)
        def _():
            wait_piece(1)
            wait_piece(2)

        pass_on(partial(0, s, bkv, None), 0, 1, s, rkv, pl.ds(0, 2 * kw))
        pass_on(partial(1, s, bkv, None), 1, 1, s, lkv, pl.ds(0, 2 * kw))

        def mlp(t, inner):
            for now in range(ntile):
                @pl.when((s == 0) & (t == now))
                def _():
                    wait_piece(3 + 2 * now)
                    wait_piece(4 + 2 * now)
                    if 5 + 2 * now + 2 < len(pieces):
                        w_remote(7 + 2 * now).start()
                        w_remote(8 + 2 * now).start()

            cols = pl.ds(pl.multiple_of(t * tw, 128), tw)
            part_g = partial(0, s, bg, cols)
            part_u = partial(1, s, bu, cols)
            pass_on(part_g, 0, 2 + t, s, rg, cols)
            pass_on(part_u, 1, 2 + t, s, lu, cols)

            @pl.when(s == nx - 1)
            def _():
                gate = rg[nx - 1, :, cols].astype(F32)
                up = lu[nx - 1, :, cols].astype(F32)
                act_out[:, cols] = (gate / (1.0 + jnp.exp(-gate)) * up).astype(BF16)

            return inner

        return lax.fori_loop(0, ntile, mlp, carry)

    lax.fori_loop(0, nx, step, 0)
    qkv_out[:, :half] = rq[nx - 1]
    qkv_out[:, half:2 * half] = lq[nx - 1]
    qkv_out[:hb, 2 * half:] = rkv[nx - 1]
    qkv_out[hb:, 2 * half:] = lkv[nx - 1]

    def sent(s, carry):
        hop(0, 0, s, rq, pl.ds(0, half)).wait_send()
        hop(1, 0, s, lq, pl.ds(0, half)).wait_send()
        hop(0, 1, s, rkv, pl.ds(0, 2 * kw)).wait_send()
        hop(1, 1, s, lkv, pl.ds(0, 2 * kw)).wait_send()
        for t in range(ntile):
            cols = pl.ds(t * tw, tw)
            hop(0, 2 + t, s, rg, cols).wait_send()
            hop(1, 2 + t, s, lu, cols).wait_send()
        return carry

    lax.fori_loop(0, nx - 1, sent, 0)


def project(nx, x_in, gain, w_q, w_k_t, w_v_t, w_gate, w_up):
    rows, hid = x_in.shape
    rb = rows // (2 * nx)
    nq, nk, nf = w_q.shape[1], w_k_t.shape[0], w_gate.shape[1]
    ntile = 3
    npiece = 3 + 2 * ntile
    vmem = pl.BlockSpec(memory_space=pltpu.VMEM)
    dma = pltpu.SemaphoreType.DMA
    return pl.pallas_call(
        functools.partial(project_kernel, nx, ntile),
        out_shape=(jax.ShapeDtypeStruct((rb, nq + 2 * nk), BF16), jax.ShapeDtypeStruct((rb, nf), BF16)),
        in_specs=[pl.BlockSpec(memory_space=ANY), vmem] + [pl.BlockSpec(memory_space=ANY)] * 5,
        out_specs=(vmem,) * 2,
        scratch_shapes=[
            pltpu.VMEM((nx, rb, 2 * hid), BF16),
            pltpu.VMEM((8, 2 * hid), F32),
            pltpu.VMEM((nx, 2 * nx, rb), F32),
            pltpu.VMEM((2 * hid, nq), BF16),
            pltpu.VMEM((2 * nk, 2 * hid), BF16),
            pltpu.VMEM((2 * hid, nf), BF16),
            pltpu.VMEM((2 * hid, nf), BF16),
            pltpu.VMEM((nx, rb, nq // 2), BF16),
            pltpu.VMEM((nx, rb // 2, 2 * nk), BF16),
            pltpu.VMEM((nx, rb, nf), BF16),
            pltpu.VMEM((nx, rb, nq // 2), BF16),
            pltpu.VMEM((nx, rb // 2, 2 * nk), BF16),
            pltpu.VMEM((nx, rb, nf), BF16),
            dma((nx,)),
            dma((nx + 1,)),
            dma((nx + 1,)),
            dma((nx - 1,)),
            dma((nx - 1,)),
            dma((npiece,)),
            dma((npiece,)),
            dma((npiece,)),
            dma((2, 2 + ntile, nx)),
            dma((2, 2 + ntile, nx)),
        ],
        compiler_params=pltpu.CompilerParams(collective_id=0, has_side_effects=True, vmem_limit_bytes=VMEM_LIMIT),
        name='project',
    )(x_in, gain, w_q, w_k_t, w_v_t, w_gate, w_up)


def swap_pairs(v):
    length = v.shape[0]
    line = lax.broadcasted_iota(jnp.int32, v.shape, 0)
    return jnp.where(lax.rem(line, 2) == 0, pltpu.roll(v, length - 1, 0), pltpu.roll(v, 1, 0))


def finish_kernel(nx, ny, heads, kv_heads, act_ref, qkv_hbm, kc_ref, vc_ref, pos_ref, qgain_ref, kgain_ref,
                  wo_ref, wd_ref, x_hbm, out_ref, k_out, v_out,
                  qkv_ref, x_ref, gbuf, gath, w2, qt, kt, vt, sc, oc, ot, kbuf, vbuf, pb, r1, mf, mq, r2,
                  c_loc, kv_loc, s_own, s_opp, s_par, recv, y1s, y1r, y2s, y2r, y3s, y3r, y4s, y4r):
    dm = lax.axis_index('dm')
    y = lax.axis_index('tp')
    xi = dm // 2
    core = lax.rem(dm, 2)
    other = 2 * xi + 1 - core
    right = lax.rem(xi + 1, nx) * 2 + core
    left = lax.rem(xi + nx - 1, nx) * 2 + core
    nf = act_ref.shape[1]
    rb = act_ref.shape[0]
    hb, qtr = rb // 2, rb // 4
    head = qgain_ref.shape[1]
    natt = heads * head
    group = heads // kv_heads
    flip, mirror = y + 1 - 2 * lax.rem(y, 2), ny - 1 - y
    p1 = flip + core * (mirror - flip)
    p2 = mirror + core * (flip - mirror)
    bit_a, bit_b, bit_c = lax.rem((y + 1) // 2, 2), y // 2, lax.rem(y, 2)
    b1 = bit_a + core * (bit_b - bit_a)
    b2 = bit_b + core * (bit_c - bit_b)

    act_cols, att_cols = pl.ds(natt, nf), pl.ds(0, natt)

    def to(peer):
        return dict(device_id={'dm': peer}, device_id_type=MESH)

    def to_y(peer):
        return dict(device_id={'tp': peer}, device_id_type=MESH)

    def own_send(n, h, kind):
        peer, slot = ((right, 4), (left, 2), (other, 1))[n]
        cols = att_cols if kind else act_cols
        src = gath.at[0, pl.ds(h * hb, hb), cols] if kind else act_ref.at[pl.ds(h * hb, hb), :]
        return pltpu.make_async_remote_copy(
            src_ref=src, dst_ref=gath.at[slot, pl.ds(h * hb, hb), cols],
            send_sem=s_own.at[n, h, kind], recv_sem=recv.at[slot, h, kind], **to(peer))

    def opp_send(n, h, kind):
        peer, slot, sem = ((right, 4, 6), (left, 2, 2 * nx))[n]
        cols = att_cols if kind else act_cols
        rows = pl.ds(h * hb + n * qtr, qtr)
        return pltpu.make_async_remote_copy(
            src_ref=gath.at[slot, rows, cols], dst_ref=gath.at[6, rows, cols],
            send_sem=s_opp.at[n, h, kind], recv_sem=recv.at[sem, h, kind], **to(peer))

    def opp_landed(n, h, kind):
        cols = att_cols if kind else act_cols
        part = gath.at[6, pl.ds(h * hb + n * qtr, qtr), cols]
        return pltpu.make_async_remote_copy(
            src_ref=part, dst_ref=part, send_sem=s_opp.at[n, h, kind], recv_sem=recv.at[(6, 2 * nx)[n], h, kind], **to(other))

    def par_send(slot, h, kind):
        cols = att_cols if kind else act_cols
        return pltpu.make_async_remote_copy(
            src_ref=gath.at[slot, pl.ds(h * hb, hb), cols], dst_ref=gath.at[slot + 1, pl.ds(h * hb, hb), cols],
            send_sem=s_par.at[slot // 2 - 1, h, kind], recv_sem=recv.at[slot + 1, h, kind], **to(other))

    def landed(slot, h, kind):
        cols = att_cols if kind else act_cols
        part = gath.at[slot, pl.ds(h * hb, hb), cols]
        return pltpu.make_async_remote_copy(
            src_ref=part, dst_ref=part, send_sem=s_own.at[0, 0, 0], recv_sem=recv.at[slot, h, kind], **to(other))

    locals_ = [pltpu.make_async_copy(act_ref, gath.at[0, :, act_cols], c_loc.at[0]),
               pltpu.make_async_copy(wo_ref, w2.at[att_cols, :], c_loc.at[1]),
               pltpu.make_async_copy(wd_ref, w2.at[act_cols, :], c_loc.at[2]),
               pltpu.make_async_copy(x_hbm, x_ref, c_loc.at[3])]
    qkv_copy = pltpu.make_async_copy(qkv_hbm, qkv_ref, c_loc.at[4])
    qkv_copy.start()

    ctx = kc_ref.shape[1]
    cs = kbuf.shape[1]
    n_chunks = ctx // cs

    def cache_copy(side, idx):
        ref, buf = ((kc_ref, kbuf), (vc_ref, vbuf))[side]
        slot = lax.rem(idx, 2)
        return pltpu.make_async_copy(ref.at[idx // n_chunks, pl.ds(lax.rem(idx, n_chunks) * cs, cs)], buf.at[slot],
                                     kv_loc.at[side, slot])

    for side in range(2):
        cache_copy(side, 0).start()

    barrier = pltpu.get_barrier_semaphore()
    for peer in (other, right, left):
        pl.semaphore_signal(barrier, inc=1, **to(peer))
    for peer in (p1, p2):
        pl.semaphore_signal(barrier, inc=1, **to_y(peer))
    pl.semaphore_wait(barrier, 5)

    for h in range(2):
        for n in range(3):
            own_send(n, h, 0).start()
    for copy in locals_:
        copy.start()

    kv_wide = kv_heads * head
    gbuf[...] = jnp.zeros(gbuf.shape, F32)
    gbuf[0:heads, 0:head] = qgain_ref[...].astype(F32)
    gbuf[heads:heads + kv_heads, 0:head] = kgain_ref[...].astype(F32)
    gain_t = jnp.transpose(gbuf[...])
    gswap_t = swap_pairs(gain_t)
    line = lax.broadcasted_iota(jnp.int32, (head, rb), 0)
    odd = lax.rem(line, 2)
    inv_freq = jnp.exp((line - odd).astype(F32) * (-math.log(ROPE_THETA) / head))
    angles = inv_freq * pos_ref[...].astype(F32)
    cos_a = jnp.cos(angles)
    sin_a = jnp.sin(angles) * (2 * odd - 1).astype(F32)
    qkv_copy.wait()
    qkv_t = jnp.transpose(qkv_ref[...].astype(F32))
    swap_t = swap_pairs(qkv_t[:natt + kv_wide])
    for n in range(heads + kv_heads):
        own = slice(n * head, (n + 1) * head)
        one, two = qkv_t[own], swap_t[own]
        mean = jnp.mean(one, axis=0, keepdims=True)
        centred = one - mean
        scale = lax.rsqrt(jnp.mean(centred * centred, axis=0, keepdims=True) + NORM_EPS)
        turned = (centred * scale * gain_t[:head, n:n + 1] * cos_a
                  + (two - mean) * scale * gswap_t[:head, n:n + 1] * sin_a)
        turned = turned.astype(BF16)
        if n < heads:
            qt[n] = turned.astype(F32)
        else:
            k_out[n - heads] = turned
            kt[n - heads] = turned.astype(F32)
    for n in range(kv_heads):
        one = qkv_t[natt + kv_wide + n * head:natt + kv_wide + (n + 1) * head]
        vt[n] = one
        v_out[n] = one.astype(BF16)

    score_scale = head ** -0.5
    db = 16

    def attend_head(kv, carry):
        first = kv * group

        def score_chunk(c, inner):
            idx = kv * n_chunks + c
            slot = lax.rem(idx, 2)
            cache_copy(0, idx).wait()

            @pl.when(idx < kv_heads * n_chunks - 1)
            def _():
                cache_copy(0, idx + 1).start()

            def score(s, deep):
                keys = kbuf[slot, s].astype(F32)
                sc[c * cs + s] = jnp.concatenate(
                    [jnp.sum(qt[first + j] * keys, axis=0, keepdims=True) for j in range(group)], axis=0)
                return deep

            return lax.fori_loop(0, cs, score, inner)

        lax.fori_loop(0, n_chunks, score_chunk, 0)
        k_one = kt[kv]
        s_one = jnp.concatenate([jnp.sum(qt[first + j] * k_one, axis=0, keepdims=True) for j in range(group)], axis=0) * score_scale
        scores = sc[...] * score_scale
        at = lax.broadcasted_iota(jnp.int32, scores.shape, 0)
        scores = jnp.where(at < pos_ref[...][None], scores, -1e30)
        top = jnp.maximum(jnp.max(scores, axis=0), s_one)
        probs = jnp.exp(scores - top[None])
        p_one = jnp.exp(s_one - top)
        denom = jnp.sum(probs, axis=0) + p_one
        sc[...] = probs.astype(BF16).astype(F32)
        v_one = vt[kv]
        for j in range(group):
            oc[j] = p_one[j:j + 1] * v_one

        def value_chunk(c, inner):
            idx = kv * n_chunks + c
            slot = lax.rem(idx, 2)
            cache_copy(1, idx).wait()

            @pl.when(idx < kv_heads * n_chunks - 1)
            def _():
                cache_copy(1, idx + 1).start()

            def value(b, deep):
                lines = pl.ds(pl.multiple_of(b * db, db), db)
                sums = [oc[j, lines, :] for j in range(group)]
                for s in range(cs):
                    vals = vbuf[slot, s, lines, :].astype(F32)
                    for j in range(group):
                        sums[j] = sums[j] + sc[c * cs + s, j:j + 1, :] * vals
                for j in range(group):
                    oc[j, lines, :] = sums[j]
                return deep

            return lax.fori_loop(0, head // db, value, inner)

        lax.fori_loop(0, n_chunks, value_chunk, 0)
        for j in range(group):
            lines = pl.ds(pl.multiple_of((first + j) * head, 8), head)
            ot[lines, :] = oc[j] / denom[j:j + 1]
        return carry

    lax.fori_loop(0, kv_heads, attend_head, 0)
    gath[0, :, 0:natt] = jnp.transpose(ot[...]).astype(BF16)
    for h in range(2):
        for n in range(3):
            own_send(n, h, 1).start()
    for copy in locals_:
        copy.wait()

    def block_rows(place, j):
        off = place + (place // 2) * (5 - 2 * place)
        who = core + j * (1 - 2 * core)
        return (lax.rem(xi + off, nx) * 2 + who) * rb

    groups = [(place, 0, rb) for place in range(nx - 1)] + [(nx - 1, 0, hb), (nx - 1, hb, hb)]

    def aligned(start, size):
        return pl.ds(pl.multiple_of(start, size), size)

    def y1(g, j):
        place, row0, size = groups[g]
        i = 2 * place + j
        return pltpu.make_async_remote_copy(
            src_ref=pb.at[i, aligned(row0 + (1 - b1) * (size // 2), size // 2), :], dst_ref=r1.at[i, pl.ds(row0 // 2, size // 2), :],
            send_sem=y1s.at[2 * g + j], recv_sem=y1r.at[2 * g + j], **to_y(p1))

    def y2(g, j):
        place, row0, size = groups[g]
        i = 2 * place + j
        rows = pl.ds(row0 // 4, size // 4)
        return pltpu.make_async_remote_copy(
            src_ref=mq.at[i, rows, :], dst_ref=r2.at[i, rows, :],
            send_sem=y2s.at[2 * g + j], recv_sem=y2r.at[2 * g + j], **to_y(p2))

    def y3(g, j, mine):
        place, row0, size = groups[g]
        quarter = b2 if mine else 1 - b2
        start = block_rows(place, j) + row0 + b1 * (size // 2) + quarter * (size // 4)
        rows = out_ref.at[aligned(start, size // 4), :]
        return pltpu.make_async_remote_copy(
            src_ref=rows, dst_ref=rows, send_sem=y3s.at[2 * g + j], recv_sem=y3r.at[2 * g + j], **to_y(p2))

    def y4(g, j, mine):
        place, row0, size = groups[g]
        half = b1 if mine else 1 - b1
        rows = out_ref.at[aligned(block_rows(place, j) + row0 + half * (size // 2), size // 2), :]
        return pltpu.make_async_remote_copy(
            src_ref=rows, dst_ref=rows, send_sem=y4s.at[2 * g + j], recv_sem=y4r.at[2 * g + j], **to_y(p1))

    def product(g, kinds=(0, 1)):
        place, row0, size = groups[g]
        rows = pl.ds(row0, size)
        if len(kinds) == 2:
            cols = slice(None)
        else:
            cols = att_cols if kinds[0] else act_cols

        def body(j, carry):
            i = 2 * place + j

            @pl.when(j == 1)
            def _():
                for kind in kinds:
                    for h in range(row0 // hb, (row0 + size) // hb):
                        landed(2 * place + 1, h, kind).wait_recv()

            part = jnp.dot(gath[i, rows, cols], w2[cols, :], preferred_element_type=F32)
            if kinds == (1,):
                part = part + mf[i, rows, :]
            mf[i, rows, :] = part
            if 1 in kinds:
                pb[i, rows, :] = part.astype(BF16)
                y1(g, j).start()
            return carry

        lax.fori_loop(0, 2, body, 0)

    def stage2(g):
        place, row0, size = groups[g]
        for j in range(2):
            i = 2 * place + j
            y1(g, j).wait_recv()
            rows = aligned(row0 + b1 * (size // 2) + (1 - b2) * (size // 4), size // 4)
            sub = aligned(row0 // 2 + (1 - b2) * (size // 4), size // 4)
            mq[i, row0 // 4:(row0 + size) // 4, :] = (mf[i, rows, :] + r1[i, sub, :].astype(F32)).astype(BF16)
            y2(g, j).start()

    def stage3(g):
        place, row0, size = groups[g]
        for j in range(2):
            i = 2 * place + j
            y2(g, j).wait_recv()
            rows = aligned(row0 + b1 * (size // 2) + b2 * (size // 4), size // 4)
            sub = aligned(row0 // 2 + b2 * (size // 4), size // 4)
            total = mf[i, rows, :] + r1[i, sub, :].astype(F32) + r2[i, row0 // 4:(row0 + size) // 4, :].astype(F32)
            rows = aligned(block_rows(place, j) + row0 + b1 * (size // 2) + b2 * (size // 4), size // 4)
            out_ref[rows, :] = (x_ref[rows, :].astype(F32) + total).astype(BF16)
            y3(g, j, True).start()

    def stage4(g):
        for j in range(2):
            y3(g, j, False).wait_recv()
            y4(g, j, True).start()

    def near_landed(kind):
        for slot in (2, 4):
            for h in range(2):
                landed(slot, h, kind).wait_recv()
        if kind == 0:
            forwards = ((0, 0),)
        else:
            forwards = ((0, 1), (1, 0), (1, 1))
        for h, k in forwards:
            for n in range(2):
                opp_send(n, h, k).start()
        for slot in (2, 4):
            for h in range(2):
                par_send(slot, h, kind).start()

    def far_landed(h, kind):
        for n in range(2):
            opp_landed(n, h, kind).wait_recv()
        par_send(6, h, kind).start()

    product(0)
    stage2(0)
    near_landed(0)
    stage3(0)
    near_landed(1)
    stage4(0)
    product(1)
    product(2)
    stage2(1)
    stage2(2)
    far_landed(0, 0)
    far_landed(0, 1)
    stage3(1)
    stage3(2)
    product(3)
    stage4(1)
    stage4(2)
    stage2(3)
    stage3(3)
    far_landed(1, 0)
    product(4, (0,))
    far_landed(1, 1)
    product(4, (1,))
    stage4(3)
    stage2(4)
    stage3(4)
    stage4(4)

    for g in range(len(groups)):
        for j in range(2):
            y4(g, j, False).wait_recv()
            y1(g, j).wait_send()
            y2(g, j).wait_send()
            y3(g, j, True).wait_send()
            y4(g, j, True).wait_send()
    for kind in range(2):
        for h in range(2):
            for n in range(3):
                own_send(n, h, kind).wait_send()
            for slot in (2, 4, 6):
                par_send(slot, h, kind).wait_send()
            for n in range(2):
                opp_send(n, h, kind).wait_send()


def finish(nx, ny, act, qkv, k_cache, v_cache, positions, q_gain, k_gain, w_out, w_down, x_in):
    rb, nf = act.shape
    kv_heads, ctx, head = k_cache.shape[:3]
    natt, wcols = w_out.shape
    heads = natt // head
    group = heads // kv_heads
    cs = 16
    vmem = pl.BlockSpec(memory_space=pltpu.VMEM)
    hbm = pl.BlockSpec(memory_space=ANY)
    dma = pltpu.SemaphoreType.DMA
    new = jax.ShapeDtypeStruct((kv_heads, head, rb), BF16)
    return pl.pallas_call(
        functools.partial(finish_kernel, nx, ny, heads, kv_heads),
        out_shape=(jax.ShapeDtypeStruct(x_in.shape, BF16), new, new),
        in_specs=[hbm, hbm, hbm, hbm, vmem, vmem, vmem, hbm, hbm, hbm],
        out_specs=(vmem, vmem, vmem),
        scratch_shapes=[
            pltpu.VMEM(qkv.shape, BF16),
            pltpu.VMEM(x_in.shape, BF16),
            pltpu.VMEM((128, pl.cdiv(head, 128) * 128), F32),
            pltpu.VMEM((2 * nx, rb, natt + nf), BF16),
            pltpu.VMEM((natt + nf, wcols), BF16),
            pltpu.VMEM((heads, head, rb), F32),
            pltpu.VMEM((kv_heads, head, rb), F32),
            pltpu.VMEM((kv_heads, head, rb), F32),
            pltpu.VMEM((ctx, group, rb), F32),
            pltpu.VMEM((group, head, rb), F32),
            pltpu.VMEM((natt, rb), F32),
            pltpu.VMEM((2, cs, head, rb), BF16),
            pltpu.VMEM((2, cs, head, rb), BF16),
            pltpu.VMEM((2 * nx, rb, wcols), BF16),
            pltpu.VMEM((2 * nx, rb // 2, wcols), BF16),
            pltpu.VMEM((2 * nx, rb, wcols), F32),
            pltpu.VMEM((2 * nx, rb // 4, wcols), BF16),
            pltpu.VMEM((2 * nx, rb // 4, wcols), BF16),
            dma((5,)),
            dma((2, 2)),
            dma((3, 2, 2)),
            dma((2, 2, 2)),
            dma((3, 2, 2)),
            dma((2 * nx + 1, 2, 2)),
        ] + [dma((2 * nx + 2,))] * 8,
        compiler_params=pltpu.CompilerParams(collective_id=1, has_side_effects=True, vmem_limit_bytes=VMEM_LIMIT),
        name='finish',
    )(act, qkv, k_cache, v_cache, positions, q_gain, k_gain, w_out, w_down, x_in)


def settle_kernel(n_parts, x_ref, k_ref, v_ref, x_out, k_out, v_out, xbuf, kbuf, vbuf, sem_in, sem_out):
    rows = x_ref.shape[0] // n_parts
    moves = [(x_ref.at[pl.ds(n * rows, rows)], xbuf.at[pl.ds(n * rows, rows)], x_out.at[pl.ds(n * rows, rows)]) for n in range(n_parts)]
    moves += [(k_ref, kbuf, k_out), (v_ref, vbuf, v_out)]
    for n, (src, mid, _) in enumerate(moves):
        pltpu.make_async_copy(src, mid, sem_in.at[n]).start()
    for n, (src, mid, dst) in enumerate(moves):
        pltpu.make_async_copy(src, mid, sem_in.at[n]).wait()
        pltpu.make_async_copy(mid, dst, sem_out.at[n]).start()
    for n, (_, mid, dst) in enumerate(moves):
        pltpu.make_async_copy(mid, dst, sem_out.at[n]).wait()


def settle(x_out, k_t, v_t):
    n_parts = 4
    hbm = pl.BlockSpec(memory_space=ANY)
    arrays = (x_out, k_t, v_t)
    return pl.pallas_call(
        functools.partial(settle_kernel, n_parts),
        out_shape=tuple(jax.ShapeDtypeStruct(a.shape, a.dtype) for a in arrays),
        in_specs=[hbm] * 3,
        out_specs=(hbm,) * 3,
        scratch_shapes=[pltpu.VMEM(a.shape, a.dtype) for a in arrays] + [pltpu.SemaphoreType.DMA((n_parts + 2,))] * 2,
        name='settle',
    )(*arrays)


def solution(mesh):
    dm_size = mesh.shape['dm']
    nx = dm_size // 2
    x_spec = P('dp', 'dm')
    row_spec = P(('dp', 'dm'))
    cache_spec = P(('dp', 'dm'), 'tp', None, None)
    new_spec = P(('dp', 'dm'), 'tp', None)
    hid_tp = P('dm', 'tp')
    tp_hid = P('tp', 'dm')
    head_spec = P('tp', None)

    def device_step(x_in, positions, k_cache, v_cache, ln_gain, w_q, w_k, w_v, w_gate, w_up, q_gain, k_gain, w_out, w_down):
        qkv, act = project(nx, x_in, ln_gain[None, :], w_q, w_k.T, w_v.T, w_gate, w_up)
        x_out, k_t, v_t = settle(*finish(
            nx, mesh.shape['tp'], act, qkv, jnp.transpose(k_cache, (1, 2, 3, 0)), jnp.transpose(v_cache, (1, 2, 3, 0)),
            positions[None, :], q_gain, k_gain, w_out, w_down, x_in))
        k_new = jnp.transpose(k_t, (2, 0, 1))
        v_new = jnp.transpose(v_t, (2, 0, 1))
        return x_out, k_new, v_new

    return jax.shard_map(
        device_step,
        mesh=mesh,
        in_specs=(x_spec, row_spec, cache_spec, cache_spec, P('dm'), hid_tp, hid_tp, hid_tp, hid_tp, hid_tp, head_spec, head_spec, tp_hid, tp_hid),
        out_specs=(x_spec, new_spec, new_spec),
        check_vma=False,
    )
```

time: 493 us -> 282 us (0.57)
  waiting for transfers between devices: 164 us -> 0 us
  Pallas kernels: 172 us -> 278 us
  local copies, waits for them, and re-layouts: 55.7 us -> 1.26 us
  matrix products: 43.5 us -> 0 us
  other arithmetic: 22.5 us -> 0 us
  blocking collectives: 19 us -> 0 us
  between operations: 14.2 us -> 0.83 us
    pallas_call x0 -> x2, Pallas kernels: none -> 113 us  [the longest x1 110 us: finish(): pl.pallas_call(functools.partial(finish_kernel, nx, ny, heads, kv_heads),...]
    all_gather x2 -> x0, waiting for transfers between devices: 102 us -> none  [the longest x1 64.4 us: device_step(): act_all = lax.all_gather(act, 'dm', axis=0, tiled=True)]
    psum x1 -> x0, waiting for transfers between devices: 61.2 us -> none  [device_step(): out_sum = lax.psum(part_out.astype(jnp.bfloat16), 'tp')]
    unnamed x30 -> x0, local copies, waits for them, and re-layouts: 48.3 us -> none
    dot_general x5 -> x0, matrix products: 43.5 us -> none  [the longest x1 17.6 us: device_step(): jnp.dot(act_all, w_down, preferred_element_type=jnp.float32)]
    all_gather x1 -> x0, blocking collectives: 19 us -> none  [device_step(): stats = lax.all_gather(jnp.stack([loc_mean, loc_m2]), 'dm', axis=0)]
    convert_element_type x4 -> x0, other arithmetic: 8.96 us -> none  [the longest x1 3.89 us: device_step(): x_out = (x_f32 + out_sum.astype(jnp.float32)).astype(jnp.bfloat16)]
    pallas_call x1, Pallas kernels: 172 us -> 165 us  [project(): pl.pallas_call(functools.partial(project_kernel, nx, ntile), out_shape=(j...]
  transfers between devices with their start and end apart: 3 -> 0, of which waited for: 3 -> 0; matrix products, arithmetic and copies ran while one was open for 2% -> 0% of each run, Pallas kernels for 0% -> 0%
where the time goes in v3:
time: 282 us; the launch traced here: 280 us
  Pallas kernels  278 us (99%)
    pallas_call x1, Pallas kernels, project(): pl.pallas_call(functools.partial(project_kernel, nx, ntile), out_shape=(j...  165 us
    pallas_call x1, Pallas kernels, finish(): pl.pallas_call(functools.partial(finish_kernel, nx, ny, heads, kv_heads),...  110 us

profile of v3, /device:TPU:97, one launch (start us, length us, event | category | flops | bytes accessed | tf_op | source)
XLA Modules:
  0.0 280.3 jit_solution(17411009706530767826)
XLA Ops:
  0.6 1.3 broadcast_in_dim.6.gain_ref
  1.9 165.1 %project.1 = (bf16[256,1920]{1,0:T(8,128)(2,1)}, bf16[256,3456]{1,0:T(8,128)(2,1)}) custom-call(bf16[2048,640]{1,0:T(8,128)(2,1)} %x_hbm.1, bf16[1,640]{1,0:T(2,128)(2,1)} %broadcast_in_dim.6.gain_ref, bf16[640,1280]{1,0:T(8,128)(2,1)} %wq_ref.1, bf16[320,640]{1,0:T(8,128)(2,1)} %bitcast.9, bf16[320,640]{1,0:T(8,128)(2,1)} %bitcast.10, ...), custom_call_target="tpu_custom_call" | custom-call | tf_op jit(solution)/shard_map/project/pallas_call | solution.py:238
  167.0 110.3 %finish.1 = (bf16[2048,640]{1,0:T(8,128)(2,1)}, bf16[2,160,256]{2,1,0:T(8,128)(2,1)}, bf16[2,160,256]{2,1,0:T(8,128)(2,1)}) custom-call(bf16[256,3456]{1,0:T(8,128)(2,1)} %get-tuple-element.11.act_ref, bf16[256,1920]{1,0:T(8,128)(2,1)} %get-tuple-element.12.qkv_hbm, bf16[2,64,160,256]{3,2,1,0:T(8,128)(2,1)} %bitcast.7, bf16[2,64,160,256]{3,2,1,0:T(8,128)(2,1)} %bitcast.8, ...), custom_call_target="tpu_custom_call" | custom-call | tf_op jit(solution)/shard_map/finish/pallas_call | solution.py:657
  277.3 2.8 settle.1

commit v4 on v3

--- a/solution.py
+++ b/solution.py
@@ -17,10 +17,10 @@
 VMEM_LIMIT = 66 * 1024 * 1000 - 1024 * 600
 
 
-def project_kernel(nx, ntile, x_ref, gain_ref, wq_ref, wk_ref, wv_ref, wg_ref, wu_ref,
+def project_kernel(nx, nload, ntile, x_ref, gain_ref, wq_ref, wk_ref, wv_ref, wg_ref, wu_ref,
                    qkv_out, act_out,
-                   xbuf, gain, stat, bq, bkv, bg, bu, rq, rkv, rg, lq, lkv, lu,
-                   x_loc, x_snd, x_rcv, t_snd, t_rcv, w_loc, w_snd, w_rcv, r_snd, r_rcv):
+                   xbuf, gain, stat, bq, bkv, bg, bu, rq, rkv, rg, lq, lkv, lu, qkv_buf, act_buf,
+                   o_sem, x_loc, x_snd, x_rcv, t_snd, t_rcv, w_loc, w_snd, w_rcv, r_snd, r_rcv):
     dm = lax.axis_index('dm')
     xi = dm // 2
     core = lax.rem(dm, 2)
@@ -31,13 +31,15 @@
     hb = rb // 2
     hid = x_ref.shape[1]
     tw = wg_ref.shape[1] // ntile
+    lw = wg_ref.shape[1] // nload
+    per = ntile // nload
 
     every = slice(None)
     kw = wk_ref.shape[0]
     pieces = [(wq_ref, bq, 0, every), (wk_ref, bkv, 1, pl.ds(0, kw)), (wv_ref, bkv, 1, pl.ds(kw, kw))]
-    for t in range(ntile):
-        pieces.append((wg_ref, bg, 0, pl.ds(t * tw, tw)))
-        pieces.append((wu_ref, bu, 0, pl.ds(t * tw, tw)))
+    for n in range(nload):
+        pieces.append((wg_ref, bg, 0, pl.ds(n * lw, lw)))
+        pieces.append((wu_ref, bu, 0, pl.ds(n * lw, lw)))
 
     def x_local(j):
         return pltpu.make_async_copy(
@@ -74,7 +76,7 @@
             src_ref=stat.at[0], dst_ref=stat.at[d], send_sem=t_snd.at[d - 1], recv_sem=t_rcv.at[d - 1],
             device_id={'dm': lax.rem(xi + d, nx) * 2 + core}, device_id_type=MESH)
 
-    gain[:, 0:hid] = jnp.broadcast_to(gain_ref[...].astype(F32), (8, hid))
+    gain[:, 0:hid] = jnp.broadcast_to(gain_ref[...].astype(F32)[None, :], (8, hid))
     for j in range(nx):
         x_local(j).start()
     for n in range(len(pieces)):
@@ -89,8 +91,7 @@
     for j in range(nx):
         x_remote(j).start()
     g_remote().start()
-    for n in range(3):
-        w_remote(n).start()
+    w_remote(0).start()
 
     for ref in (rq, rkv, rg, lq, lkv, lu):
         ref[0] = jnp.zeros(ref.shape[1:], ref.dtype)
@@ -105,7 +106,7 @@
         centred = values - mean
         both = jnp.where(lane == 2 * j, mean, both)
         both = jnp.where(lane == 2 * j + 1, jnp.sum(centred * centred, axis=1, keepdims=True), both)
-    for n in range(3, 5):
+    for n in range(1, 5):
         w_remote(n).start()
     stat[0] = jnp.transpose(both)[:2 * nx]
     for d in range(1, nx):
@@ -161,6 +162,12 @@
         w_remote(n).wait()
 
     half = rq.shape[2]
+    qkv_leave = pltpu.make_async_copy(qkv_buf, qkv_out, o_sem.at[ntile])
+
+    def act_leave(t):
+        cols = pl.ds(pl.multiple_of(t * tw, 128), tw)
+        return pltpu.make_async_copy(act_buf.at[:, cols], act_out.at[:, cols], o_sem.at[t])
+
 
     def step(s, carry):
         @pl.when(s == 0)
@@ -181,9 +188,17 @@
         pass_on(partial(0, s, bkv, None), 0, 1, s, rkv, pl.ds(0, 2 * kw))
         pass_on(partial(1, s, bkv, None), 1, 1, s, lkv, pl.ds(0, 2 * kw))
 
+        @pl.when(s == nx - 1)
+        def _():
+            qkv_buf[:, :half] = rq[nx - 1]
+            qkv_buf[:, half:2 * half] = lq[nx - 1]
+            qkv_buf[:hb, 2 * half:] = rkv[nx - 1]
+            qkv_buf[hb:, 2 * half:] = lkv[nx - 1]
+            qkv_leave.start()
+
         def mlp(t, inner):
-            for now in range(ntile):
-                @pl.when((s == 0) & (t == now))
+            for now in range(nload):
+                @pl.when((s == 0) & (t == now * per))
                 def _():
                     wait_piece(3 + 2 * now)
                     wait_piece(4 + 2 * now)
@@ -201,45 +216,50 @@
             def _():
                 gate = rg[nx - 1, :, cols].astype(F32)
                 up = lu[nx - 1, :, cols].astype(F32)
-                act_out[:, cols] = (gate / (1.0 + jnp.exp(-gate)) * up).astype(BF16)
+                act_buf[:, cols] = (gate / (1.0 + jnp.exp(-gate)) * up).astype(BF16)
+                act_leave(t).start()
 
             return inner
 
         return lax.fori_loop(0, ntile, mlp, carry)
 
     lax.fori_loop(0, nx, step, 0)
-    qkv_out[:, :half] = rq[nx - 1]
-    qkv_out[:, half:2 * half] = lq[nx - 1]
-    qkv_out[:hb, 2 * half:] = rkv[nx - 1]
-    qkv_out[hb:, 2 * half:] = lkv[nx - 1]
-
     def sent(s, carry):
         hop(0, 0, s, rq, pl.ds(0, half)).wait_send()
         hop(1, 0, s, lq, pl.ds(0, half)).wait_send()
         hop(0, 1, s, rkv, pl.ds(0, 2 * kw)).wait_send()
         hop(1, 1, s, lkv, pl.ds(0, 2 * kw)).wait_send()
-        for t in range(ntile):
-            cols = pl.ds(t * tw, tw)
+        def sent_mlp(t, inner):
+            cols = pl.ds(pl.multiple_of(t * tw, 128), tw)
             hop(0, 2 + t, s, rg, cols).wait_send()
             hop(1, 2 + t, s, lu, cols).wait_send()
+            return inner
+
+        return lax.fori_loop(0, ntile, sent_mlp, carry)
+
+    lax.fori_loop(0, nx - 1, sent, 0)
+    qkv_leave.wait()
+
+    def left_all(t, carry):
+        act_leave(t).wait()
         return carry
 
-    lax.fori_loop(0, nx - 1, sent, 0)
+    lax.fori_loop(0, ntile, left_all, 0)
 
 
 def project(nx, x_in, gain, w_q, w_k_t, w_v_t, w_gate, w_up):
     rows, hid = x_in.shape
     rb = rows // (2 * nx)
     nq, nk, nf = w_q.shape[1], w_k_t.shape[0], w_gate.shape[1]
-    ntile = 3
-    npiece = 3 + 2 * ntile
+    nload, ntile = 3, 9
+    npiece = 3 + 2 * nload
     vmem = pl.BlockSpec(memory_space=pltpu.VMEM)
     dma = pltpu.SemaphoreType.DMA
     return pl.pallas_call(
-        functools.partial(project_kernel, nx, ntile),
+        functools.partial(project_kernel, nx, nload, ntile),
         out_shape=(jax.ShapeDtypeStruct((rb, nq + 2 * nk), BF16), jax.ShapeDtypeStruct((rb, nf), BF16)),
         in_specs=[pl.BlockSpec(memory_space=ANY), vmem] + [pl.BlockSpec(memory_space=ANY)] * 5,
-        out_specs=(vmem,) * 2,
+        out_specs=(pl.BlockSpec(memory_space=ANY),) * 2,
         scratch_shapes=[
             pltpu.VMEM((nx, rb, 2 * hid), BF16),
             pltpu.VMEM((8, 2 * hid), F32),
@@ -254,6 +274,9 @@
             pltpu.VMEM((nx, rb, nq // 2), BF16),
             pltpu.VMEM((nx, rb // 2, 2 * nk), BF16),
             pltpu.VMEM((nx, rb, nf), BF16),
+            pltpu.VMEM((rb, nq + 2 * nk), BF16),
+            pltpu.VMEM((rb, nf), BF16),
+            dma((ntile + 1,)),
             dma((nx,)),
             dma((nx + 1,)),
             dma((nx + 1,)),
@@ -277,8 +300,8 @@
 
 
 def finish_kernel(nx, ny, heads, kv_heads, act_ref, qkv_hbm, kc_ref, vc_ref, pos_ref, qgain_ref, kgain_ref,
-                  wo_ref, wd_ref, x_hbm, out_ref, k_out, v_out,
-                  qkv_ref, x_ref, gbuf, gath, w2, qt, kt, vt, sc, oc, ot, kbuf, vbuf, pb, r1, mf, mq, r2,
+                  wo_ref, wd_ref, x_hbm, out_hbm, k_hbm, v_hbm,
+                  out_ref, k_out, v_out, o_sem, qkv_ref, x_ref, gbuf, gath, w2, qt, kt, vt, sc, oc, ot, kbuf, vbuf, pb, r1, mf, mq, r2,
                   c_loc, kv_loc, s_own, s_opp, s_par, recv, y1s, y1r, y2s, y2r, y3s, y3r, y4s, y4r):
     dm = lax.axis_index('dm')
     y = lax.axis_index('tp')
@@ -409,6 +432,10 @@
         vt[n] = one
         v_out[n] = one.astype(BF16)
 
+    new_leave = (pltpu.make_async_copy(k_out, k_hbm, o_sem.at[0]), pltpu.make_async_copy(v_out, v_hbm, o_sem.at[1]))
+    for copy in new_leave:
+        copy.start()
+
     score_scale = head ** -0.5
     db = 16
 
@@ -577,6 +604,16 @@
         for j in range(2):
             y3(g, j, False).wait_recv()
             y4(g, j, True).start()
+
+    def leave(g, j):
+        place, row0, size = groups[g]
+        rows = aligned(block_rows(place, j) + row0, size)
+        return pltpu.make_async_copy(out_ref.at[rows, :], out_hbm.at[rows, :], o_sem.at[2 + 2 * g + j])
+
+    def settled(g):
+        for j in range(2):
+            y4(g, j, False).wait_recv()
+            leave(g, j).start()
 
     def near_landed(kind):
         for slot in (2, 4):
@@ -619,6 +656,8 @@
     stage3(3)
     far_landed(1, 0)
     product(4, (0,))
+    for g in range(nx - 1):
+        settled(g)
     far_landed(1, 1)
     product(4, (1,))
     stage4(3)
@@ -626,13 +665,17 @@
     stage3(4)
     stage4(4)
 
+    for g in range(nx - 1, len(groups)):
+        settled(g)
     for g in range(len(groups)):
         for j in range(2):
-            y4(g, j, False).wait_recv()
+            leave(g, j).wait()
             y1(g, j).wait_send()
             y2(g, j).wait_send()
             y3(g, j, True).wait_send()
             y4(g, j, True).wait_send()
+    for copy in new_leave:
+        copy.wait()
     for kind in range(2):
         for h in range(2):
             for n in range(3):
@@ -658,8 +701,12 @@
         functools.partial(finish_kernel, nx, ny, heads, kv_heads),
         out_shape=(jax.ShapeDtypeStruct(x_in.shape, BF16), new, new),
         in_specs=[hbm, hbm, hbm, hbm, vmem, vmem, vmem, hbm, hbm, hbm],
-        out_specs=(vmem, vmem, vmem),
+        out_specs=(hbm, hbm, hbm),
         scratch_shapes=[
+            pltpu.VMEM(x_in.shape, BF16),
+            pltpu.VMEM(new.shape, BF16),
+            pltpu.VMEM(new.shape, BF16),
+            dma((2 + 4 * nx,)),
             pltpu.VMEM(qkv.shape, BF16),
             pltpu.VMEM(x_in.shape, BF16),
             pltpu.VMEM((128, pl.cdiv(head, 128) * 128), F32),
@@ -729,7 +776,7 @@
     head_spec = P('tp', None)
 
     def device_step(x_in, positions, k_cache, v_cache, ln_gain, w_q, w_k, w_v, w_gate, w_up, q_gain, k_gain, w_out, w_down):
-        qkv, act = project(nx, x_in, ln_gain[None, :], w_q, w_k.T, w_v.T, w_gate, w_up)
+        qkv, act = project(nx, x_in, ln_gain, w_q, w_k.T, w_v.T, w_gate, w_up)
         x_out, k_t, v_t = settle(*finish(
             nx, mesh.shape['tp'], act, qkv, jnp.transpose(k_cache, (1, 2, 3, 0)), jnp.transpose(v_cache, (1, 2, 3, 0)),
             positions[None, :], q_gain, k_gain, w_out, w_down, x_in))

time: 282 us -> 279 us (0.989)
  no operation moved by 1% of the time
where the time goes in v4:
time: 279 us; the launch traced here: 278 us
  Pallas kernels  278 us (100%)
    pallas_call x1, Pallas kernels, project(): pl.pallas_call(functools.partial(project_kernel, nx, nload, ntile), out_s...  164 us
    pallas_call x1, Pallas kernels, finish(): pl.pallas_call(functools.partial(finish_kernel, nx, ny, heads, kv_heads),...  111 us

profile of v4, /device:TPU:97, one launch (start us, length us, event | category | flops | bytes accessed | tf_op | source)
XLA Modules:
  0.0 278.3 jit_solution(7753373749025225168)
XLA Ops:
  0.6 163.8 %project.1 = (bf16[256,1920]{1,0:T(8,128)(2,1)}, bf16[256,3456]{1,0:T(8,128)(2,1)}) custom-call(bf16[2048,640]{1,0:T(8,128)(2,1)} %x_hbm.1, bf16[640]{0:T(1024)(128)(2,1)} %gain_ref.1, bf16[640,1280]{1,0:T(8,128)(2,1)} %wq_ref.1, bf16[320,640]{1,0:T(8,128)(2,1)} %bitcast.9, bf16[320,640]{1,0:T(8,128)(2,1)} %bitcast.10, bf16[640,3456]{1,0:T(8,128)(2,1)} %wg_ref.1, ...), custom_call_target="tpu_custom_call" | custom-call | tf_op jit(solution)/shard_map/project/pallas_call | solution.py:258
  164.4 110.9 %finish.1 = (bf16[2048,640]{1,0:T(8,128)(2,1)}, bf16[2,160,256]{2,1,0:T(8,128)(2,1)}, bf16[2,160,256]{2,1,0:T(8,128)(2,1)}) custom-call(bf16[256,3456]{1,0:T(8,128)(2,1)} %get-tuple-element.11.act_ref, bf16[256,1920]{1,0:T(8,128)(2,1)} %get-tuple-element.12.qkv_hbm, bf16[2,64,160,256]{3,2,1,0:T(8,128)(2,1)} %bitcast.7, bf16[2,64,160,256]{3,2,1,0:T(8,128)(2,1)} %bitcast.8, ...), custom_call_target="tpu_custom_call" | custom-call | tf_op jit(solution)/shard_map/finish/pallas_call | solution.py:700
  275.4 2.8 settle.1

commit v5 on v4

--- a/solution.py
+++ b/solution.py
@@ -302,7 +302,7 @@
 def finish_kernel(nx, ny, heads, kv_heads, act_ref, qkv_hbm, kc_ref, vc_ref, pos_ref, qgain_ref, kgain_ref,
                   wo_ref, wd_ref, x_hbm, out_hbm, k_hbm, v_hbm,
                   out_ref, k_out, v_out, o_sem, qkv_ref, x_ref, gbuf, gath, w2, qt, kt, vt, sc, oc, ot, kbuf, vbuf, pb, r1, mf, mq, r2,
-                  c_loc, kv_loc, s_own, s_opp, s_par, recv, y1s, y1r, y2s, y2r, y3s, y3r, y4s, y4r):
+                  c_loc, kv_loc, s_own, s_opp, s_par, recv, y1s, y1r, y2s, y2r, y3s, y3r, y4s, y4r, y5s, y5r):
     dm = lax.axis_index('dm')
     y = lax.axis_index('tp')
     xi = dm // 2
@@ -319,9 +319,11 @@
     flip, mirror = y + 1 - 2 * lax.rem(y, 2), ny - 1 - y
     p1 = flip + core * (mirror - flip)
     p2 = mirror + core * (flip - mirror)
+    p3 = lax.rem(y + 2, ny)
     bit_a, bit_b, bit_c = lax.rem((y + 1) // 2, 2), y // 2, lax.rem(y, 2)
     b1 = bit_a + core * (bit_b - bit_a)
     b2 = bit_b + core * (bit_c - bit_b)
+    q1 = b2 + core * (1 - 2 * b2)
 
     act_cols, att_cols = pl.ds(natt, nf), pl.ds(0, natt)
 
@@ -388,9 +390,9 @@
     barrier = pltpu.get_barrier_semaphore()
     for peer in (other, right, left):
         pl.semaphore_signal(barrier, inc=1, **to(peer))
-    for peer in (p1, p2):
+    for peer in (p1, p2, p3):
         pl.semaphore_signal(barrier, inc=1, **to_y(peer))
-    pl.semaphore_wait(barrier, 5)
+    pl.semaphore_wait(barrier, 6)
 
     for h in range(2):
         for n in range(3):
@@ -543,12 +545,25 @@
         return pltpu.make_async_remote_copy(
             src_ref=rows, dst_ref=rows, send_sem=y3s.at[2 * g + j], recv_sem=y3r.at[2 * g + j], **to_y(p2))
 
+    last = len(groups) - 1
+
     def y4(g, j, mine):
         place, row0, size = groups[g]
-        half = b1 if mine else 1 - b1
-        rows = out_ref.at[aligned(block_rows(place, j) + row0 + half * (size // 2), size // 2), :]
+        start = block_rows(place, j) + row0 + (b1 if mine else 1 - b1) * (size // 2)
+        count = size // 2
+        if g == last:
+            start = start + (b2 if mine else q1) * (size // 4)
+            count = size // 4
+        rows = out_ref.at[aligned(start, count), :]
         return pltpu.make_async_remote_copy(
             src_ref=rows, dst_ref=rows, send_sem=y4s.at[2 * g + j], recv_sem=y4r.at[2 * g + j], **to_y(p1))
+
+    def y5(j, mine):
+        place, row0, size = groups[last]
+        start = block_rows(place, j) + row0 + (b1 if mine else 1 - b1) * (size // 2) + (b2 if mine else 1 - q1) * (size // 4)
+        rows = out_ref.at[aligned(start, size // 4), :]
+        return pltpu.make_async_remote_copy(
+            src_ref=rows, dst_ref=rows, send_sem=y5s.at[j], recv_sem=y5r.at[j], **to_y(p3))
 
     def product(g, kinds=(0, 1)):
         place, row0, size = groups[g]
@@ -599,6 +614,9 @@
             rows = aligned(block_rows(place, j) + row0 + b1 * (size // 2) + b2 * (size // 4), size // 4)
             out_ref[rows, :] = (x_ref[rows, :].astype(F32) + total).astype(BF16)
             y3(g, j, True).start()
+            if g == last:
+                y5(j, True).start()
+                y4(g, j, True).start()
 
     def stage4(g):
         for j in range(2):
@@ -612,6 +630,9 @@
 
     def settled(g):
         for j in range(2):
+            if g == last:
+                y3(g, j, False).wait_recv()
+                y5(j, False).wait_recv()
             y4(g, j, False).wait_recv()
             leave(g, j).start()
 
@@ -653,8 +674,8 @@
     stage4(1)
     stage4(2)
     stage2(3)
+    far_landed(1, 0)
     stage3(3)
-    far_landed(1, 0)
     product(4, (0,))
     for g in range(nx - 1):
         settled(g)
@@ -663,7 +684,6 @@
     stage4(3)
     stage2(4)
     stage3(4)
-    stage4(4)
 
     for g in range(nx - 1, len(groups)):
         settled(g)
@@ -674,6 +694,8 @@
             y2(g, j).wait_send()
             y3(g, j, True).wait_send()
             y4(g, j, True).wait_send()
+    for j in range(2):
+        y5(j, True).wait_send()
     for copy in new_leave:
         copy.wait()
     for kind in range(2):
@@ -731,7 +753,7 @@
             dma((2, 2, 2)),
             dma((3, 2, 2)),
             dma((2 * nx + 1, 2, 2)),
-        ] + [dma((2 * nx + 2,))] * 8,
+        ] + [dma((2 * nx + 2,))] * 8 + [dma((2,))] * 2,
         compiler_params=pltpu.CompilerParams(collective_id=1, has_side_effects=True, vmem_limit_bytes=VMEM_LIMIT),
         name='finish',
     )(act, qkv, k_cache, v_cache, positions, q_gain, k_gain, w_out, w_down, x_in)

time: 279 us -> 277 us (level)
  no operation moved by 1% of the time
where the time goes in v5:
time: 277 us
  Pallas kernels  276 us (100%)
    pallas_call x1, Pallas kernels, project(): pl.pallas_call(functools.partial(project_kernel, nx, nload, ntile), out_s...  164 us
    pallas_call x1, Pallas kernels, finish(): pl.pallas_call(functools.partial(finish_kernel, nx, ny, heads, kv_heads),...  109 us

profile of v5, /device:TPU:97, one launch (start us, length us, event | category | flops | bytes accessed | tf_op | source)
XLA Modules:
  0.0 276.8 jit_solution(5291145112402353396)
XLA Ops:
  0.6 163.8 %project.1 = (bf16[256,1920]{1,0:T(8,128)(2,1)}, bf16[256,3456]{1,0:T(8,128)(2,1)}) custom-call(bf16[2048,640]{1,0:T(8,128)(2,1)} %x_hbm.1, bf16[640]{0:T(1024)(128)(2,1)} %gain_ref.1, bf16[640,1280]{1,0:T(8,128)(2,1)} %wq_ref.1, bf16[320,640]{1,0:T(8,128)(2,1)} %bitcast.9, bf16[320,640]{1,0:T(8,128)(2,1)} %bitcast.10, bf16[640,3456]{1,0:T(8,128)(2,1)} %wg_ref.1, ...), custom_call_target="tpu_custom_call" | custom-call | tf_op jit(solution)/shard_map/project/pallas_call | solution.py:258
  164.4 109.4 %finish.1 = (bf16[2048,640]{1,0:T(8,128)(2,1)}, bf16[2,160,256]{2,1,0:T(8,128)(2,1)}, bf16[2,160,256]{2,1,0:T(8,128)(2,1)}) custom-call(bf16[256,3456]{1,0:T(8,128)(2,1)} %get-tuple-element.11.act_ref, bf16[256,1920]{1,0:T(8,128)(2,1)} %get-tuple-element.12.qkv_hbm, bf16[2,64,160,256]{3,2,1,0:T(8,128)(2,1)} %bitcast.7, bf16[2,64,160,256]{3,2,1,0:T(8,128)(2,1)} %bitcast.8, ...), custom_call_target="tpu_custom_call" | custom-call | tf_op jit(solution)/shard_map/finish/pallas_call | solution.py:722
  273.8 2.8 %settle.1 = (bf16[2048,640]{1,0:T(8,128)(2,1)}, bf16[2,160,256]{2,1,0:T(8,128)(2,1)}, bf16[2,160,256]{2,1,0:T(8,128)(2,1)}) custom-call(bf16[2048,640]{1,0:T(8,128)(2,1)} %get-tuple-element.13.x_ref, bf16[2,160,256]{2,1,0:T(8,128)(2,1)} %get-tuple-element.14.k_ref, bf16[2,160,256]{2,1,0:T(8,128)(2,1)} %get-tuple-element.15.v_ref), custom_call_target="tpu_custom_call" | custom-call | tf_op jit(solution)/shard_map/settle/pallas_call | solution.py:779
